TPU v7x, 128 devices: a whole 4x4x4 slice. The times are simulated.
128 devices in a mesh: row: 16 (over y, x_lo, core), col: 8 (over x_hi, z).
Axes of the slice: x: 4 (x_hi: 2, x_lo: 2; x = x_hi * 2 + x_lo), y: 4, z: 4, core: 2. Of those that a mesh axis runs over, the one named last changes fastest.
Arguments:
- adjacency: int32 [10240, 320], P('row', 'col'), may hold values from -2147483648 to 2147483647, as said below
- relabel: int32 [10240], P(('row', 'col')), may hold values from 0 to 10239, each once
Outputs:
- clustering: float32 [10240], P(('row', 'col'))
- transitivity: float32 [], replicated
Inputs may be any that keep to these rules, and one draw needn't show every extreme that they name: The unpacked adjacency is symmetric with a zero diagonal.
All inputs are finite; a program needn't handle non-finite values.
Results may differ from a plain program's by a relative error of at most 0.0003.
Values sent between devices are 32-bit elements.
A program may use at most 128 MiB of HBM per device.

v0:
```python
import jax
import jax.numpy as jnp
from jax import lax
from jax.sharding import PartitionSpec as P


def sent_to_all(value, axis):
    peers = lax.axis_size(axis)
    return lax.all_to_all(
        jnp.broadcast_to(value[None], (peers, *value.shape)), axis, 0, 0, tiled=True
    )


def laid_out(tiles, dim):
    tiles = jnp.moveaxis(tiles, 0, dim)
    dims = tiles.shape
    return tiles.reshape(*dims[:dim], dims[dim] * dims[dim + 1], *dims[dim + 2 :])


def gathered_copies(value, axis, dim):
    tiles = sent_to_all(value, axis)
    return laid_out(tiles, dim)


def cut_along(value, dim, peers):
    before, after = (value.shape[:dim], value.shape[dim + 1 :])
    return jnp.moveaxis(value.reshape(*before, peers, -1, *after), dim, 0)


def summed_on_arrival(value, axis, dim):
    tiles = cut_along(value, dim, lax.axis_size(axis))
    arrived = lax.all_to_all(tiles, axis, split_axis=0, concat_axis=0, tiled=True)
    return arrived.sum(axis=0)


def over_pieces(value, axis):
    return lax.all_gather(value, axis).sum(0)


def unpack(words):
    shifts = jnp.arange(32, dtype=jnp.int32)
    bits = lax.shift_right_logical(words[:, :, None], shifts[None, None, :]) & 1
    return bits.reshape(words.shape[0], words.shape[1] * 32).astype(jnp.bfloat16)


def body(adjacency, relabel):
    local = unpack(adjacency)
    row_block = unpack(gathered_copies(adjacency, "col", 1))
    paths = jnp.dot(
        row_block,
        unpack(lax.all_gather(adjacency, "row", axis=0, tiled=True)),
        preferred_element_type=jnp.float32,
    )
    wide = local.astype(jnp.float32)
    partial_value = jnp.sum(wide * paths, axis=1)
    degree_part = jnp.sum(wide, axis=1)
    closed, degree = (
        summed_on_arrival(partial_value, "col", 0),
        summed_on_arrival(degree_part, "col", 0),
    )
    wedges = jnp.maximum(degree * (degree - 1.0), 1.0)
    everyone = lax.all_gather(closed / wedges, ("row", "col"), axis=0, tiled=True)
    clustering = jnp.take(everyone, relabel, axis=0)
    sum_closed, sum_wedges = (
        over_pieces(jnp.sum(closed), ("row", "col")),
        over_pieces(jnp.sum(wedges), ("row", "col")),
    )
    transitivity = sum_closed / sum_wedges
    return (clustering, transitivity)


def solution(mesh):
    placed = (P("row", "col"), P(("row", "col")))
    return jax.shard_map(
        body, mesh=mesh, in_specs=placed, out_specs=(P(("row", "col")), P()), check_vma=False
    )
```

profile of v0, /device:TPU:1, one launch (start us, length us, event | category | flops | bytes accessed | tf_op | source)
XLA Modules:
  0.0 179.7 jit_solution(8041186109363718358)
XLA Ops:
  7.2 0.0 all-gather.2.cloned.1.call-start
  7.2 0.7 all-gather.2.cloned.1.call-update
  7.9 1.9 %broadcast_in_dim.8 = s32[8,640,40]{1,2,0:T(8,128)} broadcast(s32[640,40]{0,1:T(8,128)} %param.2), dimensions={1,2} | broadcast | bytes 921600 | tf_op jit(solution)/shard_map/broadcast_in_dim | solution.py:10
  9.7 8.3 %all-to-all-start = ((s32[8,640,40]{1,2,0:T(8,128)}), s32[8,640,40]{1,2,0:T(8,128)}, u32[]{:S(2)}, u32[]{:S(2)}) async-start(s32[8,640,40]{1,2,0:T(8,128)} %broadcast_in_dim.8), calls=%async_computation | async-start | bytes 1638400 | tf_op jit(solution)/shard_map/all_to_all | solution.py:9
  18.1 1.4 convert_reduce_fusion
  19.5 0.7 all_to_all.18
  20.2 0.1 shift_right_logical.72
  20.3 1.1 shift_right_logical.69
  21.4 3.0 %copy.9 = s32[640,1280]{1,0:T(8,128)} copy(s32[640,1280]{0,1:T(8,128)S(1)} %bitcast.14) | data formatting | bytes 6553600 | tf_op jit(solution)/shard_map/shift_right_logical | solution.py:42
  24.4 0.7 compare_select_fusion
  25.0 7.4 %all-to-all-done = s32[8,640,40]{1,2,0:T(8,128)} async-done(((s32[8,640,40]{1,2,0:T(8,128)}), s32[8,640,40]{1,2,0:T(8,128)}, u32[]{:S(2)}, u32[]{:S(2)}) %all-to-all-start) | async-done | bytes 819232 | tf_op jit(solution)/shard_map/all_to_all | solution.py:9
  32.4 3.9 %all-to-all-start.2 = ((f32[8,1,80]{2,1,0:T(1,128)}), f32[8,1,80]{2,1,0:T(1,128)S(1)}, u32[]{:S(2)}, u32[]{:S(2)}) async-start(f32[8,1,80]{2,1,0:T(1,128)} %all_to_all.18), calls=%async_computation.2 | async-start | bytes 8192 | tf_op jit(solution)/shard_map/all_to_all | solution.py:32
  36.3 10.3 %and_convert_fusion.1 = bf16[640,320,32]{0,2,1:T(8,128)(2,1)} fusion(s32[640,320]{0,1:T(8,128)} %bitcast.2), kind=kLoop, calls=%fused_computation.2 | loop fusion | flops 19660800 | bytes 13926400 | tf_op jit(solution)/shard_map/convert_element_type | solution.py:43
  46.6 0.8 all-gather.2.cloned.1.call-done
  47.5 0.0 copy-start
  47.5 14.2 %and_convert_fusion = bf16[10240,40,32]{0,2,1:T(8,128)(2,1)} fusion(s32[10240,40]{0,1:T(8,128)} %all-gather.2.cloned.1.call-done), kind=kLoop, calls=%fused_computation.1 | loop fusion | flops 39321600 | bytes 27852800 | tf_op jit(solution)/shard_map/convert_element_type | solution.py:43
  61.7 0.0 copy-done
  61.7 0.0 copy-start.1
  61.7 21.8 %fusion = f32[640]{0:T(1024)S(1)} fusion(bf16[640,10240]{0,1:T(8,128)(2,1)S(1)} %bitcast.15, bf16[10240,1280]{0,1:T(8,128)(2,1)} %bitcast.13, s32[640,1280]{1,0:T(8,128)} %copy.9, s32[1280]{0:T(1024)S(1)} %shift_right_logical.72), kind=kOutput, calls=%fused_computation.7 | convolution fusion | flops 16782130176 | bytes 42606080 | tf_op jit(solution)/shard_map/dot_general | solution.py:49
  83.4 0.7 all_to_all.16
  84.1 0.0 all-to-all-done.2
  84.1 6.1 %all-to-all-start.1 = ((f32[8,1,80]{2,1,0:T(1,128)}), f32[8,1,80]{2,1,0:T(1,128)S(1)}, u32[]{:S(2)}, u32[]{:S(2)}) async-start(f32[8,1,80]{2,1,0:T(1,128)} %all_to_all.16), calls=%async_computation.1 | async-start | bytes 8192 | tf_op jit(solution)/shard_map/all_to_all | solution.py:32
  90.3 6.5 %all-to-all-done.1 = f32[8,1,80]{2,1,0:T(1,128)S(1)} async-done(((f32[8,1,80]{2,1,0:T(1,128)}), f32[8,1,80]{2,1,0:T(1,128)S(1)}, u32[]{:S(2)}, u32[]{:S(2)}) %all-to-all-start.1) | async-done | bytes 2592 | tf_op jit(solution)/shard_map/all_to_all | solution.py:32
  96.8 0.6 fusion.3
  97.4 0.7 fusion.2
  98.1 0.8 dynamic-update-slice.2
  98.8 0.8 dynamic-update-slice.1
  99.6 67.8 %all-reduce.3 = (f32[10240]{0:T(1024)S(1)}, f32[128]{0:T(128)S(1)}, f32[128]{0:T(128)S(1)}) all-reduce(f32[10240]{0:T(1024)S(1)} %get-tuple-element.8, f32[128]{0:T(128)S(1)} %dynamic-update-slice.1, f32[128]{0:T(128)S(1)} %dynamic-update-slice.2), channel_id=1, replica_groups=mesh['row'=16,'col'=8] {'row','col'}, use_global_device_ids=true, to_apply=%add | all-reduce | flops 10496 | bytes 83968
  167.4 1.1 gather_fusion
  168.5 0.0 copy-done.1
  168.5 0.5 and_select_fusion
  169.0 0.7 reduce_sum.79
  169.7 0.6 reduce_sum.77
  (6 shorter events, 0.0 us)
Async XLA Ops:
  7.2 40.3 %all-gather.2.cloned.1.call-start = ((), (), s32[]{:S(2)}) async-start(), calls=%async_computation.3 | async-start | bytes 1740800 | tf_op jit(solution)/shard_map/all_gather | solution.py:51
  9.7 22.7 %all-to-all-start = ((s32[8,640,40]{1,2,0:T(8,128)}), s32[8,640,40]{1,2,0:T(8,128)}, u32[]{:S(2)}, u32[]{:S(2)}) async-start(s32[8,640,40]{1,2,0:T(8,128)} %broadcast_in_dim.8), calls=%async_computation | async-start | bytes 1638400 | tf_op jit(solution)/shard_map/all_to_all | solution.py:9
  32.4 51.7 %all-to-all-start.2 = ((f32[8,1,80]{2,1,0:T(1,128)}), f32[8,1,80]{2,1,0:T(1,128)S(1)}, u32[]{:S(2)}, u32[]{:S(2)}) async-start(f32[8,1,80]{2,1,0:T(1,128)} %all_to_all.18), calls=%async_computation.2 | async-start | bytes 8192 | tf_op jit(solution)/shard_map/all_to_all | solution.py:32
  47.5 14.2 %copy-start = (bf16[640,320,32]{0,2,1:T(8,128)(2,1)S(1)}, bf16[640,320,32]{0,2,1:T(8,128)(2,1)}, u32[]{:S(2)}) copy-start(bf16[640,320,32]{0,2,1:T(8,128)(2,1)} %and_convert_fusion.1) | copy-start | bytes 39321604
  61.7 106.8 %copy-start.1 = (s32[80]{0:T(128)S(1)}, s32[80]{0:T(128)}, u32[]{:S(2)}) copy-start(s32[80]{0:T(128)} %param.3) | copy-start | bytes 964
  84.1 12.7 %all-to-all-start.1 = ((f32[8,1,80]{2,1,0:T(1,128)}), f32[8,1,80]{2,1,0:T(1,128)S(1)}, u32[]{:S(2)}, u32[]{:S(2)}) async-start(f32[8,1,80]{2,1,0:T(1,128)} %all_to_all.16), calls=%async_computation.1 | async-start | bytes 8192 | tf_op jit(solution)/shard_map/all_to_all | solution.py:32
Sparse Core Ops, SparseCore 0:
  9.6 37.8 all-gather.1
where the time goes:
time: 180 us
  blocking collectives  67.8 us (38%)
  other arithmetic  29.7 us (16%)
  matrix products  21.8 us (12%)
  starting transfers between devices  18.3 us (10%)
  between operations  16.6 us (9%)
  waiting for transfers between devices  15.4 us (9%)
  local copies, waits for them, and re-layouts  10.1 us (6%)
    unnamed x1, blocking collectives  67.8 us
    convert_element_type x2, other arithmetic, unpack(): bits.reshape(words.shape[0], words.shape[1] * 32).astype(jnp.bfloat16)  24.5 us
    dot_general x1, matrix products, body(): jnp.dot(row_block, unpack(lax.all_gather(adjacency, 'row', axis=0, tiled=...  21.8 us
    all_to_all x2, starting transfers between devices, summed_on_arrival(): lax.all_to_all(tiles, axis, split_axis=0, concat_axis=0, tiled=True)  9.99 us
    all_to_all x1, starting transfers between devices, sent_to_all(): lax.all_to_all(jnp.broadcast_to(value[None], (peers, *value.shape)), axis...  8.31 us
    all_to_all x1, waiting for transfers between devices, sent_to_all(): lax.all_to_all(jnp.broadcast_to(value[None], (peers, *value.shape)), axis...  7.4 us
    all_to_all x2, waiting for transfers between devices, summed_on_arrival(): lax.all_to_all(tiles, axis, split_axis=0, concat_axis=0, tiled=True)  6.5 us
    shift_right_logical x4, local copies, waits for them, and re-layouts, unpack(): bits = lax.shift_right_logical(words[:, :, None], shifts[None, None, :]) & 1  4.2 us
  transfers between devices with their start and end apart: 4, of which 3 were waited for; matrix products, arithmetic and copies ran while one was open for 30% of the time, Pallas kernels for 0%

commit v1 on v0

v1 whole, which is shorter than its diff:
```python
import jax
import jax.numpy as jnp
from jax import lax
from jax.experimental import pallas as pl
from jax.experimental.pallas import tpu as pltpu
from jax.sharding import PartitionSpec as P

G0 = (0, 4, 1, 5, 6, 2, 7, 3)
G1 = (0, 7, 6, 1, 3, 4, 5, 2)
E0 = (0, 2, 5, 7, 1, 3, 4, 6)
E1 = (0, 3, 7, 4, 5, 6, 2, 1)
F8 = jnp.float8_e4m3fn
I32 = jnp.int32
WORDS, ROWS, WIDE = 40, 640, 1280
TILE = 256


def look_up(table, d):
    return sum(jnp.where(d == i, I32(v), I32(0)) for i, v in enumerate(table) if v)


def xor3(a, b):
    out = I32(0)
    for bit in (1, 2, 4):
        p, q = (a // bit) % 2, (b // bit) % 2
        out = out + bit * (p + q - 2 * p * q)
    return out


def bits_of(row, mask, kind):
    wide = jnp.broadcast_to(row, (32, row.shape[1]))
    return jnp.where((wide & mask) != 0, 1.0, 0.0).astype(kind)


def kernel(
    adj, rel, out,
    own, rhs, lhs, w_rhs, w_lhs, acc, part_row, part_col, red_row, red_col, mine, every,
    send, rhs_sem, lhs_sem, relay_sem, row_sem, col_sem, all_send, all_sem,
):
    row, col = lax.axis_index("row"), lax.axis_index("col")
    R, C, h = row // 2, col, row % 2
    d = xor3(R, C)
    diag, off = d == 0, d != 0

    barrier = pltpu.get_barrier_semaphore()

    def hello(r, c):
        pl.semaphore_signal(barrier, inc=1, device_id={"row": r, "col": c})

    @pl.loop(1, 8)
    def _(i):
        for g in range(2):
            hello(2 * R + g, (C + i) % 8)
            hello(2 * ((R + i) % 8) + g, C)

    hello(2 * R + 1 - h, C)
    own[...] = adj[...].T

    @pl.when(diag)
    def _():
        lhs[2, h] = own[...]

    pl.semaphore_wait(barrier, 29)

    def copy(src, dst, ssem, rsem, r, c):
        return pltpu.make_async_remote_copy(
            src_ref=src, dst_ref=dst, send_sem=ssem, recv_sem=rsem,
            device_id={"row": r, "col": c},
        )

    def relay(s):
        return copy(lhs.at[s, h], lhs.at[s, h], send.at[7 + s], relay_sem.at[s], 2 * R + 1 - h, C)

    offers = []
    for j, (g, e) in enumerate(((G0, E0), (G1, E1))):
        to = xor3(R, xor3(d, look_up(g, d)))
        offers.append(copy(own, rhs.at[1 - j], send.at[2 * j], rhs_sem.at[1 - j], row, to))
        to = xor3(C, look_up(e, d))
        offers.append(
            copy(own, lhs.at[j, h], send.at[2 * j + 1], lhs_sem.at[j], 2 * to + h, C)
        )

    spread = [
        copy(own, lhs.at[2, h], send.at[i - 1], lhs_sem.at[2], 2 * ((R + i) % 8) + h, C)
        for i in range(1, 8)
    ]

    @pl.when(off)
    def _():
        for c in offers:
            c.start()

    @pl.when(diag)
    def _():
        for c in spread:
            c.start()
        relay(2).start()

    mask = jnp.left_shift(I32(1), lax.broadcasted_iota(I32, (32, ROWS), 0))

    def unpack_rhs(src):
        @pl.loop(0, 5)
        def _(i):
            base = pl.multiple_of(i * 8, 8)
            for w in range(8):
                at = pl.multiple_of(i * 256 + w * 32, 32)
                w_rhs[pl.ds(at, 32), :] = bits_of(src[pl.ds(base + w, 1), :], mask, F8)

    def product(s, first):
        @pl.loop(0, WIDE // TILE)
        def _(i):
            base = pl.multiple_of(i * (TILE // 32), TILE // 32)
            for g in range(2):
                for w in range(TILE // 32):
                    w_lhs[w * 32 : (w + 1) * 32, g * ROWS : (g + 1) * ROWS] = bits_of(
                        lhs[s, g, pl.ds(base + w, 1), :], mask, F8
                    )
            at = pl.ds(pl.multiple_of(i * TILE, TILE), TILE)
            part = jnp.dot(w_lhs[...], w_rhs[...], preferred_element_type=jnp.float32)
            if first:
                acc[at, :] = part
            else:
                acc[at, :] += part

    @pl.when(off)
    def _():
        for s in range(2):
            copy(own, rhs.at[s], send.at[0], rhs_sem.at[s], row, col).wait_recv()
            unpack_rhs(rhs.at[s])
            copy(own, lhs.at[s, h], send.at[0], lhs_sem.at[s], row, col).wait_recv()
            relay(s).start()
            copy(own, lhs.at[s, 1 - h], send.at[0], relay_sem.at[s], row, col).wait_recv()
            product(s, s == 0)
        copy(own, lhs.at[2, h], send.at[0], lhs_sem.at[2], row, col).wait_recv()
        relay(2).start()

    @pl.when(diag)
    def _():
        acc[...] = jnp.zeros_like(acc)

    unpack_rhs(own)
    copy(own, lhs.at[2, 1 - h], send.at[0], relay_sem.at[2], row, col).wait_recv()
    product(2, False)

    zero = jnp.zeros((1, ROWS), jnp.float32)

    def fold(i, carry):
        closed, degree = carry
        base = pl.multiple_of(i * 8, 8)
        for q in range(2):
            sums = []
            for w in range(4):
                at = pl.multiple_of(i * 256 + q * 128 + w * 32, 32)
                bit = bits_of(own[pl.ds(base + q * 4 + w, 1), :], mask, jnp.float32)
                val = bit * acc[pl.ds(at, 32), :]
                closed = closed + jnp.sum(val.reshape(4, 8, ROWS), axis=0)
                degree = degree + jnp.sum(bit.reshape(4, 8, ROWS), axis=0)
                sums.append(sum(val[:, k * 128 : (k + 1) * 128] for k in range(5)))
            across = jnp.concatenate(sums, axis=0).T
            part_col[2 * i + q, :, :] = 2.0 * jnp.sum(across, axis=0, keepdims=True)
        return closed, degree

    closed, degree = lax.fori_loop(
        0, 5, fold, (jnp.zeros((8, ROWS), jnp.float32), jnp.zeros((8, ROWS), jnp.float32))
    )
    closed = jnp.sum(closed, axis=0, keepdims=True)
    degree = jnp.sum(degree, axis=0, keepdims=True)
    for k in range(5):
        part_row[k, :, :] = closed[:, k * 128 : (k + 1) * 128]
        part_row[5 + k, :, :] = degree[:, k * 128 : (k + 1) * 128]

    give_row = copy(part_row, red_row.at[C], send.at[10], row_sem.at[C], row, R)
    give_col = [
        copy(
            part_col.at[pl.ds(5 * g, 5)], red_col.at[R, h], send.at[11 + g],
            col_sem.at[R, h], 2 * C + g, C,
        )
        for g in range(2)
    ]

    @pl.when(off)
    def _():
        give_row.start()
        for c in give_col:
            c.start()
        for c in offers:
            c.wait_send()
        for s in range(2):
            relay(s).wait_send()
        relay(2).wait_send()
        give_row.wait_send()
        for c in give_col:
            c.wait_send()

    def tell(i):
        to = (row * 8 + col + i) % 128
        return copy(mine, every.at[row], all_send.at[i], all_sem.at[row], to // 8, to % 8)

    @pl.when(diag)
    def _():
        for c in spread:
            c.wait_send()
        relay(2).wait_send()
        tot = part_row[...]

        def add(i, tot):
            o = (R + i) % 8
            copy(part_row, red_row.at[o], send.at[0], row_sem.at[o], row, col).wait_recv()
            tot = tot + red_row[o]
            both = jnp.zeros((5, 1, 128), jnp.float32)
            for g in range(2):
                copy(
                    part_col.at[pl.ds(0, 5)], red_col.at[o, g], send.at[0],
                    col_sem.at[o, g], row, col,
                ).wait_recv()
                both = both + red_col[o, g]
            return tot + jnp.concatenate([both, jnp.zeros_like(both)], axis=0)

        tot = lax.fori_loop(1, 8, add, tot)
        total, deg = tot[:5, 0, :], tot[5:, 0, :]
        wedges = jnp.maximum(deg * (deg - 1.0), 1.0)
        mine[0:5, :] = total / wedges
        mine[5:6, :] = jnp.sum(total, axis=0, keepdims=True)
        mine[6:7, :] = jnp.sum(wedges, axis=0, keepdims=True)
        mine[7:8, :] = jnp.zeros((1, 128), jnp.float32)
        every[row] = mine[...]

        @pl.loop(1, 128)
        def _(i):
            tell(i).start()

    def arrived(b):
        @pl.when((R != C) | (row != b))
        def _():
            copy(mine, every.at[b], all_send.at[0], all_sem.at[b], row, col).wait_recv()

    for b in range(16):
        arrived(b)

    want = jnp.broadcast_to(rel[...], (8, 128))
    block, rest = want // ROWS, want % ROWS
    line, lane = rest // 128, rest % 128
    here = lax.broadcasted_iota(I32, (8, 128), 0) == line
    found = jnp.zeros((8, 128), jnp.float32)
    sums = jnp.zeros((8, 128), jnp.float32)
    for b in range(16):
        tile = every[b]
        sums = sums + tile
        got = jnp.take_along_axis(tile, lane, axis=1)
        found = found + jnp.where(here & (block == b), got, 0.0)
    ratio = jnp.sum(sums[5:6, :], axis=1, keepdims=True) / jnp.sum(
        sums[6:7, :], axis=1, keepdims=True
    )
    out[0:1, :] = jnp.sum(found, axis=0, keepdims=True)
    out[1:2, :] = jnp.broadcast_to(ratio, (1, 128))

    @pl.when(diag)
    def _():
        @pl.loop(1, 128)
        def _(i):
            tell(i).wait_send()


def body(adjacency, relabel):
    f32 = jnp.float32
    dma = pltpu.SemaphoreType.DMA
    wanted = jnp.pad(relabel, (0, 48))[None, :]
    out = pl.pallas_call(
        kernel,
        out_shape=jax.ShapeDtypeStruct((2, 128), f32),
        in_specs=[pl.BlockSpec(memory_space=pltpu.VMEM)] * 2,
        out_specs=pl.BlockSpec(memory_space=pltpu.VMEM),
        scratch_shapes=[
            pltpu.VMEM((WORDS, ROWS), I32),
            pltpu.VMEM((2, WORDS, ROWS), I32),
            pltpu.VMEM((3, 2, WORDS, ROWS), I32),
            pltpu.VMEM((WIDE, ROWS), F8),
            pltpu.VMEM((TILE, WIDE), F8),
            pltpu.VMEM((WIDE, ROWS), f32),
            pltpu.VMEM((10, 1, 128), f32),
            pltpu.VMEM((10, 1, 128), f32),
            pltpu.VMEM((8, 10, 1, 128), f32),
            pltpu.VMEM((8, 2, 5, 1, 128), f32),
            pltpu.VMEM((8, 128), f32),
            pltpu.VMEM((16, 8, 128), f32),
            dma((13,)),
            dma((2,)),
            dma((3,)),
            dma((3,)),
            dma((8,)),
            dma((8, 2)),
            dma((128,)),
            dma((16,)),
        ],
        compiler_params=pltpu.CompilerParams(
            collective_id=0, has_side_effects=True, vmem_limit_bytes=48 * 2**20
        ),
    )(adjacency, wanted)
    return out[0, :80], out[1, 0]


def solution(mesh):
    placed = (P("row", "col"), P(("row", "col")))
    return jax.shard_map(
        body, mesh=mesh, in_specs=placed, out_specs=(P(("row", "col")), P()), check_vma=False
    )
```

time: 180 us -> 47.4 us (0.26)
  blocking collectives: 67.8 us -> 0 us
  Pallas kernels: 0 us -> 43.9 us
  other arithmetic: 29.7 us -> 0 us
  matrix products: 21.8 us -> 0 us
  starting transfers between devices: 18.3 us -> 0 us
  between operations: 16.6 us -> 0.64 us
  waiting for transfers between devices: 15.4 us -> 0 us
  local copies, waits for them, and re-layouts: 10.1 us -> 2.74 us
    unnamed x1 -> x0, blocking collectives: 67.8 us -> none
    pallas_call x0 -> x1, Pallas kernels: none -> 43.9 us  [body(): pl.pallas_call(kernel, out_shape=jax.ShapeDtypeStruct((2, 128), f32), in_...]
    convert_element_type x2 -> x0, other arithmetic: 24.5 us -> none  [unpack(): bits.reshape(words.shape[0], words.shape[1] * 32).astype(jnp.bfloat16)]
    dot_general x1 -> x0, matrix products: 21.8 us -> none  [body(): jnp.dot(row_block, unpack(lax.all_gather(adjacency, 'row', axis=0, tiled=...]
    all_to_all x3 -> x0, starting transfers between devices: 18.3 us -> none  [the longest x2 9.99 us: summed_on_arrival(): lax.all_to_all(tiles, axis, split_axis=0, concat_axis=0, tiled=True)]
    all_to_all x3 -> x0, waiting for transfers between devices: 13.9 us -> none  [the longest x1 7.4 us: sent_to_all(): lax.all_to_all(jnp.broadcast_to(value[None], (peers, *value.shape)), axis...]
    shift_right_logical x4 -> x0, local copies, waits for them, and re-layouts: 4.2 us -> none  [unpack(): bits = lax.shift_right_logical(words[:, :, None], shifts[None, None, :]) & 1]
    reduce_sum x6 -> x0, other arithmetic: 4.04 us -> none  [the longest x1 1.45 us: body(): degree_part = jnp.sum(wide, axis=1)]
  transfers between devices with their start and end apart: 4 -> 0, of which waited for: 3 -> 0; matrix products, arithmetic and copies ran while one was open for 30% -> 0% of each run, Pallas kernels for 0% -> 0%
where the time goes in v1:
time: 47.4 us; the launch traced here: 47.3 us
  Pallas kernels  43.9 us (93%)
  local copies, waits for them, and re-layouts  2.74 us (6%)
  between operations  0.64 us (1%)
    pallas_call x1, Pallas kernels, body(): pl.pallas_call(kernel, out_shape=jax.ShapeDtypeStruct((2, 128), f32), in_...  43.9 us
    unnamed x1, local copies, waits for them, and re-layouts  1.05 us

profile of v1, /device:TPU:1, one launch (start us, length us, event | category | flops | bytes accessed | tf_op | source)
XLA Modules:
  0.0 47.3 jit_solution(8447538187406031194)
XLA Ops:
  0.6 0.7 %pad_bitcast_fusion.rel = s32[1,128]{1,0:T(1,128)S(1)} fusion(s32[80]{0:T(128)} %param.3), kind=kLoop, calls=%fused_computation.1 | loop fusion | bytes 832 | tf_op jit(solution)/shard_map/broadcast_in_dim | solution.py:267
  1.3 1.1 %copy.4.adj = s32[640,40]{1,0:T(8,128)S(1)} copy(s32[640,40]{0,1:T(8,128)} %param.2) | data formatting | bytes 204800 | tf_op args[0]
  2.3 43.9 %shard_map.41 = f32[2,128]{1,0:T(2,128)S(1)} custom-call(s32[640,40]{1,0:T(8,128)S(1)} %copy.4.adj, s32[1,128]{1,0:T(1,128)S(1)} %pad_bitcast_fusion.rel), custom_call_target="tpu_custom_call" | custom-call | tf_op jit(solution)/shard_map/pallas_call | solution.py:268
  46.2 0.5 %slice.7 = f32[1,1]{1,0:T(1,128)} slice(f32[2,128]{1,0:T(2,128)S(1)} %shard_map.41), slice={[1:2], [0:1]} | slice | bytes 8 | tf_op jit(solution)/shard_map/slice | solution.py:299
  46.8 0.5 %slice_bitcast_fusion = f32[80]{0:T(128)} fusion(f32[2,128]{1,0:T(2,128)S(1)} %shard_map.41), kind=kLoop, calls=%fused_computation | loop fusion | bytes 640 | tf_op jit(solution)/shard_map/squeeze | solution.py:299

commit v2 on v0

v2 whole, which is shorter than its diff:
```python
import jax
import jax.numpy as jnp
from jax import lax
from jax.experimental import pallas as pl
from jax.experimental.pallas import tpu as pltpu
from jax.sharding import PartitionSpec as P

SENDS_A = (
    148879702, 171848828, 263397976, 238957692, 196967528, 255419081, 162998856, 188054224,
    180303480, 140426066, 247412344, 254943324, 263741645, 188513900, 196376788, 154544204,
    246620752, 255602804, 207534942, 188493940, 146221632, 171409112, 180320352, 238773953,
    264057456, 238166100, 196948592, 215988570, 179731676, 137766980, 247096517, 171866724,
    255029992, 247098073, 196289112, 146367552, 224112966, 229669992, 154889812, 205403244,
    238774493, 263352556, 137913924, 187834460, 221347436, 232436546, 213857896, 163212368,
    179511888, 163275840, 146568928, 263745233, 137981524, 222048356, 207270734, 213022816,
    154822212, 171057236, 255421653, 138245348, 230503008, 146304080, 204700260, 215724362,
)
SENDS_B = (
    2012494, 0, 0, 0, 0, 0, 0, 0,
    0, 2078538, 0, 0, 0, 0, 0, 0,
    0, 0, 1877830, 0, 0, 0, 0, 0,
    0, 0, 0, 1942850, 0, 0, 0, 0,
    0, 0, 0, 0, 2010966, 0, 0, 0,
    0, 0, 0, 0, 0, 2075986, 0, 0,
    0, 0, 0, 0, 0, 0, 1551218, 0,
    0, 0, 0, 0, 0, 0, 0, 1485174,
)
KIND = (
    0, 1, 0, 1, 0, 1, 0, 0,
    1, 0, 1, 0, 1, 0, 0, 0,
    0, 1, 0, 1, 0, 0, 0, 1,
    1, 0, 1, 0, 0, 0, 1, 0,
    0, 1, 0, 0, 0, 1, 0, 1,
    1, 0, 0, 0, 1, 0, 1, 0,
    0, 0, 0, 1, 0, 1, 0, 1,
    0, 0, 1, 0, 1, 0, 1, 0,
)

F8 = jnp.float8_e4m3fn
I32 = jnp.int32
F32 = jnp.float32
WORDS, ROWS, WIDE = 40, 640, 1280
TALL = 640
X, Y, Z = 4, 4, 4


def look_up(table, d):
    return sum(jnp.where(d == i, I32(v), I32(0)) for i, v in enumerate(table) if v)


def bit_set(row, mask):
    return (jnp.broadcast_to(row, (32, row.shape[1])) & mask) != 0


def ones(row, mask):
    return jnp.where(bit_set(row, mask), 1.0, 0.0).astype(F8)


def kernel(
    adj, rel, out, ratio_out,
    own, inbox, w_rhs, w_lhs, acc, part_row, part_col, red_row, red_col, mine, every, want_ref,
    adj_sem, send, relay_sem, in_sem, row_sem, col_sem, all_send, all_sem,
):
    row, col = lax.axis_index("row"), lax.axis_index("col")
    R, C, h = row // 2, col, row % 2
    g = 1 - h
    diag, off = R == C, R != C
    fetch = pltpu.make_async_copy(adj, own, adj_sem)
    fetch.start()

    barrier = pltpu.get_barrier_semaphore()

    def hello(r, c):
        pl.semaphore_signal(barrier, inc=1, device_id={"row": r, "col": c})

    for i in range(1, 8):
        hello(row, (C + i) % 8)
        hello(2 * ((R + i) % 8) + h, C)
    hello(2 * R + g, C)

    place = R * 8 + C
    kind = look_up(KIND, place)
    codes_a, codes_b = look_up(SENDS_A, place), look_up(SENDS_B, place)
    lhs_is_own = diag | (kind == 1)
    rhs_is_own = kind == 0

    mask = jnp.left_shift(I32(1), lax.broadcasted_iota(I32, (32, ROWS), 0))
    fetch.wait()

    @pl.when(lhs_is_own)
    def _():
        inbox[7 + h] = own[...]

    @pl.when(rhs_is_own)
    def _():
        inbox[2] = own[...]

    pl.semaphore_wait(barrier, 15)

    def copy(src, dst, ssem, rsem, r, c):
        return pltpu.make_async_remote_copy(
            src_ref=src, dst_ref=dst, send_sem=ssem, recv_sem=rsem,
            device_id={"row": r, "col": c},
        )

    def offer(i):
        code = (codes_a if i < 4 else codes_b) // (128 ** (i % 4)) % 128
        slot, to, down = code % 4, code // 4 % 8, code // 32 % 2
        box = jnp.where(down == 1, 3 + 2 * slot + h, slot)
        r = jnp.where(down == 1, 2 * to + h, row)
        c = jnp.where(down == 1, col, to)
        return code >= 64, copy(own, inbox.at[box], send.at[i], in_sem.at[box], r, c)

    for i in range(7):
        there, c = offer(i)
        pl.when(there)(c.start)

    def relay(s):
        box = 3 + 2 * s + h
        return copy(inbox.at[box], inbox.at[box], relay_sem.at[s], in_sem.at[box], 2 * R + g, C)

    def arrived(box):
        copy(own, inbox.at[box], send.at[0], in_sem.at[box], row, col).wait_recv()

    def pass_on(s):
        @pl.when((s < 2) | jnp.logical_not(lhs_is_own))
        def _():
            arrived(3 + 2 * s + h)

        relay(s).start()

    first = jnp.where(diag, 2, 0)
    pass_on(first)
    acc[...] = jnp.zeros_like(acc)

    def unpack(box, to):
        @pl.loop(0, 5)
        def _(i):
            base = pl.multiple_of(i * 8, 8)
            for w in range(8):
                to(
                    pl.ds(pl.multiple_of(i * 256 + w * 32, 32), 32),
                    ones(inbox[box, pl.ds(base + w, 1), :], mask),
                )

    def to_rhs(at, value):
        w_rhs[at, :] = value

    def to_lhs(k):
        def put(at, value):
            w_lhs[at, k * ROWS : (k + 1) * ROWS] = value
        return put

    @pl.loop(first, 3)
    def _(s):
        @pl.when((s < 2) | jnp.logical_not(rhs_is_own))
        def _():
            arrived(s)

        unpack(s, to_rhs)

        @pl.when(s < 2)
        def _():
            pass_on(s + 1)

        def half(k):
            @pl.when(k == g)
            def _():
                arrived(3 + 2 * s + k)

            unpack(3 + 2 * s + k, to_lhs(k))

        half(0)
        half(1)

        @pl.loop(0, WIDE // TALL)
        def _(i):
            at = pl.ds(pl.multiple_of(i * TALL, TALL), TALL)
            acc[at, :] += jnp.dot(w_lhs[at, :], w_rhs[...], preferred_element_type=F32)

    def fold(i, carry):
        closed, degree = carry
        base = pl.multiple_of(i * 8, 8)
        for q in range(2):
            sums = []
            for w in range(4):
                at = pl.multiple_of(i * 256 + q * 128 + w * 32, 32)
                bit = bit_set(own[pl.ds(base + q * 4 + w, 1), :], mask)
                val = jnp.where(bit, acc[pl.ds(at, 32), :], 0.0)
                one = jnp.where(bit, 1.0, 0.0)
                closed = closed + jnp.sum(val.reshape(4, 8, ROWS), axis=0)
                degree = degree + jnp.sum(one.reshape(4, 8, ROWS), axis=0)
                sums.append(sum(val[:, k * 128 : (k + 1) * 128] for k in range(5)))
            across = jnp.concatenate(sums, axis=0).T
            part_col[2 * i + q, :, :] = jnp.sum(across, axis=0, keepdims=True)
        return closed, degree

    zeros = jnp.zeros((8, ROWS), F32)
    closed, degree = lax.fori_loop(0, 5, fold, (zeros, zeros))
    once_more = kind.astype(F32)
    closed = jnp.sum(closed, axis=0, keepdims=True) * (1.0 + once_more)
    degree = jnp.sum(degree, axis=0, keepdims=True)
    part_col[...] = part_col[...] * (2.0 - once_more)
    for k in range(5):
        part_row[k, :, :] = closed[:, k * 128 : (k + 1) * 128]
        part_row[5 + k, :, :] = degree[:, k * 128 : (k + 1) * 128]

    give_row = copy(part_row, red_row.at[C], send.at[7], row_sem.at[C], row, R)
    give_col = [
        copy(
            part_col.at[pl.ds(5 * k, 5)], red_col.at[R, h], send.at[8 + k],
            col_sem.at[R, h], 2 * C + k, C,
        )
        for k in range(2)
    ]

    @pl.when(off)
    def _():
        give_row.start()
        for c in give_col:
            c.start()

    def tell(dx, i, k):
        x, y, z = C // 4 * 2 + R % 2, R // 2, C % 4
        x, y, z = (x + dx) % X, (y + 2 + i // 4) % Y, (z + 2 + i % 4) % Z
        r, c = y * 4 + x % 2 * 2 + k, x // 2 * 4 + z
        return copy(mine, every.at[row], all_send.at[r * 8 + c], all_sem.at[row], r, c)

    HOME = 10

    def for_all(act):
        for dx in (2, 1, 3, 0):
            @pl.loop(0, 16)
            def _(i):
                @pl.when((i != HOME) | (dx != 0))
                def _():
                    for k in range(2):
                        act(tell(dx, i, k))
        act(tell(0, HOME, g))

    @pl.when(diag)
    def _():
        tot = part_row[...]

        def add(i, tot):
            o = (R + i) % 8
            copy(part_row, red_row.at[o], send.at[0], row_sem.at[o], row, col).wait_recv()
            tot = tot + red_row[o]
            both = jnp.zeros((5, 1, 128), F32)
            for k in range(2):
                copy(
                    part_col.at[pl.ds(0, 5)], red_col.at[o, k], send.at[0],
                    col_sem.at[o, k], row, col,
                ).wait_recv()
                both = both + red_col[o, k]
            return tot + jnp.concatenate([both, jnp.zeros_like(both)], axis=0)

        tot = lax.fori_loop(1, 8, add, tot)
        total, deg = tot[:5, 0, :], tot[5:, 0, :]
        wedges = jnp.maximum(deg * (deg - 1.0), 1.0)
        mine[0:5, :] = total / wedges
        low = lax.broadcasted_iota(I32, (1, 128), 1) < 64
        both = []
        for v in (total, wedges):
            v = jnp.sum(v, axis=0, keepdims=True)
            both.append(v + pltpu.roll(v, 64, 1))
        mine[5:6, :] = jnp.where(low, both[0], both[1])
        every[row] = mine[...]
        for_all(lambda c: c.start())

    want_ref[...] = jnp.zeros_like(want_ref)
    want_ref[:, 0:80] = rel[...]
    want = jnp.broadcast_to(want_ref[...], (6, 128))
    block, rest = want // ROWS, want % ROWS
    line, lane = rest // 128, rest % 128
    here = lax.broadcasted_iota(I32, (6, 128), 0) == line

    for i in range(7):
        there, c = offer(i)
        pl.when(there)(c.wait_send)

    @pl.loop(first, 3)
    def _(s):
        relay(s).wait_send()

    @pl.when(off)
    def _():
        give_row.wait_send()
        for c in give_col:
            c.wait_send()

    found = jnp.zeros((6, 128), F32)
    sums = jnp.zeros((1, 128), F32)
    for b in range(16):
        @pl.when(off | (row != b))
        def _():
            copy(mine, every.at[b], all_send.at[0], all_sem.at[b], row, col).wait_recv()

        tile = every[b]
        sums = sums + tile[5:6, :]
        got = jnp.take_along_axis(tile, lane, axis=1)
        found = found + jnp.where(here & (block == b), got, 0.0)
    low = lax.broadcasted_iota(I32, (1, 128), 1) < 64
    top = jnp.sum(jnp.where(low, sums, 0.0), axis=1, keepdims=True)
    bottom = jnp.sum(jnp.where(low, 0.0, sums), axis=1, keepdims=True)
    ratio_out[...] = top / bottom
    out[...] = jnp.sum(found, axis=0, keepdims=True)[:, 0:80]

    @pl.when(diag)
    def _():
        for_all(lambda c: c.wait_send())


def body(adjacency, relabel):
    dma = pltpu.SemaphoreType.DMA
    vmem = pltpu.VMEM
    out, ratio = pl.pallas_call(
        kernel,
        out_shape=(jax.ShapeDtypeStruct((1, 80), F32), jax.ShapeDtypeStruct((1, 1), F32)),
        in_specs=[pl.BlockSpec(memory_space=pl.ANY), pl.BlockSpec(memory_space=vmem)],
        out_specs=[pl.BlockSpec(memory_space=vmem)] * 2,
        scratch_shapes=[
            vmem((WORDS, ROWS), I32),
            vmem((9, WORDS, ROWS), I32),
            vmem((WIDE, ROWS), F8),
            vmem((WIDE, WIDE), F8),
            vmem((WIDE, ROWS), F32),
            vmem((10, 1, 128), F32),
            vmem((10, 1, 128), F32),
            vmem((8, 10, 1, 128), F32),
            vmem((8, 2, 5, 1, 128), F32),
            vmem((6, 128), F32),
            vmem((16, 6, 128), F32),
            vmem((1, 128), I32),
            dma,
            dma((10,)),
            dma((3,)),
            dma((9,)),
            dma((8,)),
            dma((8, 2)),
            dma((128,)),
            dma((16,)),
        ],
        compiler_params=pltpu.CompilerParams(
            collective_id=0, has_side_effects=True, vmem_limit_bytes=48 * 2**20
        ),
    )(adjacency.T, relabel[None, :])
    return out[0], ratio[0, 0]


def solution(mesh):
    placed = (P("row", "col"), P(("row", "col")))
    return jax.shard_map(
        body, mesh=mesh, in_specs=placed, out_specs=(P(("row", "col")), P()), check_vma=False
    )
```

time: 180 us -> 48.8 us (0.27)
  blocking collectives: 67.8 us -> 0 us
  Pallas kernels: 0 us -> 44.2 us
  other arithmetic: 29.7 us -> 0 us
  matrix products: 21.8 us -> 0 us
  starting transfers between devices: 18.3 us -> 0 us
  waiting for transfers between devices: 15.4 us -> 0 us
  between operations: 16.6 us -> 2.41 us
  local copies, waits for them, and re-layouts: 10.1 us -> 2.06 us
    unnamed x1 -> x0, blocking collectives: 67.8 us -> none
    pallas_call x0 -> x1, Pallas kernels: none -> 44.2 us  [body(): pl.pallas_call(kernel, out_shape=(jax.ShapeDtypeStruct((1, 80), F32), jax...]
    convert_element_type x2 -> x0, other arithmetic: 24.5 us -> none  [unpack(): bits.reshape(words.shape[0], words.shape[1] * 32).astype(jnp.bfloat16)]
    dot_general x1 -> x0, matrix products: 21.8 us -> none  [body(): jnp.dot(row_block, unpack(lax.all_gather(adjacency, 'row', axis=0, tiled=...]
    all_to_all x3 -> x0, starting transfers between devices: 18.3 us -> none  [the longest x2 9.99 us: summed_on_arrival(): lax.all_to_all(tiles, axis, split_axis=0, concat_axis=0, tiled=True)]
    all_to_all x3 -> x0, waiting for transfers between devices: 13.9 us -> none  [the longest x1 7.4 us: sent_to_all(): lax.all_to_all(jnp.broadcast_to(value[None], (peers, *value.shape)), axis...]
    shift_right_logical x4 -> x0, local copies, waits for them, and re-layouts: 4.2 us -> none  [unpack(): bits = lax.shift_right_logical(words[:, :, None], shifts[None, None, :]) & 1]
    reduce_sum x6 -> x0, other arithmetic: 4.04 us -> none  [the longest x1 1.45 us: body(): degree_part = jnp.sum(wide, axis=1)]
  transfers between devices with their start and end apart: 4 -> 0, of which waited for: 3 -> 0; matrix products, arithmetic and copies ran while one was open for 30% -> 0% of each run, Pallas kernels for 0% -> 0%
where the time goes in v2:
time: 48.8 us; the launch traced here: 48.7 us
  Pallas kernels  44.2 us (91%)
  between operations  2.41 us (5%)
  local copies, waits for them, and re-layouts  2.06 us (4%)
    pallas_call x1, Pallas kernels, body(): pl.pallas_call(kernel, out_shape=(jax.ShapeDtypeStruct((1, 80), F32), jax...  44.2 us
    unnamed x5, local copies, waits for them, and re-layouts  2.06 us

profile of v2, /device:TPU:1, one launch (start us, length us, event | category | flops | bytes accessed | tf_op | source)
XLA Modules:
  0.0 48.7 jit_solution(17911459286130710322)
XLA Ops:
  0.6 0.0 copy-start.1
  0.6 0.6 %copy-done.1 = s32[80]{0:T(128)S(1)} copy-done((s32[80]{0:T(128)S(1)}, s32[80]{0:T(128)}, u32[]{:S(2)}) %copy-start.1) | copy-done | bytes 344
  1.3 0.0 copy-start
  1.3 0.9 %copy-done = s32[640,40]{0,1:T(8,128)S(1)} copy-done((s32[640,40]{0,1:T(8,128)S(1)}, s32[640,40]{0,1:T(8,128)}, u32[]{:S(2)}) %copy-start) | copy-done | bytes 102424
  2.2 44.2 %shard_map.41 = (f32[1,80]{1,0:T(1,128)S(1)}, f32[1,1]{1,0:T(1,128)}) custom-call(s32[40,640]{1,0:T(8,128)S(1)} %bitcast.4, s32[1,80]{1,0:T(1,128)S(1)} %bitcast.5), custom_call_target="tpu_custom_call" | custom-call | tf_op jit(solution)/shard_map/pallas_call | solution.py:317
  46.4 0.5 %copy.6 = f32[80]{0:T(128)} copy(f32[80]{0:T(128)S(1)} %bitcast.6) | data formatting | bytes 640
Async XLA Ops:
  0.6 0.7 %copy-start.1 = (s32[80]{0:T(128)S(1)}, s32[80]{0:T(128)}, u32[]{:S(2)}) copy-start(s32[80]{0:T(128)} %param.3) | copy-start | bytes 964
  1.3 0.9 %copy-start = (s32[640,40]{0,1:T(8,128)S(1)}, s32[640,40]{0,1:T(8,128)}, u32[]{:S(2)}) copy-start(s32[640,40]{0,1:T(8,128)} %param.2) | copy-start | bytes 307204

commit v3 on v2

--- a/solution.py
+++ b/solution.py
@@ -6,66 +6,69 @@
 from jax.sharding import PartitionSpec as P
 
 SENDS_A = (
-    148879702, 171848828, 263397976, 238957692, 196967528, 255419081, 162998856, 188054224,
-    180303480, 140426066, 247412344, 254943324, 263741645, 188513900, 196376788, 154544204,
-    246620752, 255602804, 207534942, 188493940, 146221632, 171409112, 180320352, 238773953,
-    264057456, 238166100, 196948592, 215988570, 179731676, 137766980, 247096517, 171866724,
-    255029992, 247098073, 196289112, 146367552, 224112966, 229669992, 154889812, 205403244,
-    238774493, 263352556, 137913924, 187834460, 221347436, 232436546, 213857896, 163212368,
-    179511888, 163275840, 146568928, 263745233, 137981524, 222048356, 207270734, 213022816,
-    154822212, 171057236, 255421653, 138245348, 230503008, 146304080, 204700260, 215724362,
+    257605490, 171605116, 163537496, 1866856, 197031157, 146367608, 179465804, 229911156,
+    180303480, 266059126, 1801844, 155082844, 138375372, 230452348, 221587568, 187983560,
+    146040436, 238973044, 199012726, 205355132, 137833028, 1539792, 180121724, 162930800,
+    247427696, 154493040, 247036152, 190690162, 1469048, 137766980, 146220148, 171801828,
+    163476709, 180186216, 146171484, 263201380, 257603426, 138310764, 196831816, 1604712,
+    171734748, 263742572, 254877792, 154169048, 146749032, 266057062, 2061924, 188377164,
+    171123284, 1275584, 146307180, 196225120, 179334756, 205158500, 165458278, 238645356,
+    1204840, 171057236, 179514468, 137983220, 213613152, 187787360, 247034088, 157135714,
 )
 SENDS_B = (
-    2012494, 0, 0, 0, 0, 0, 0, 0,
-    0, 2078538, 0, 0, 0, 0, 0, 0,
-    0, 0, 1877830, 0, 0, 0, 0, 0,
-    0, 0, 0, 1942850, 0, 0, 0, 0,
-    0, 0, 0, 0, 2010966, 0, 0, 0,
-    0, 0, 0, 0, 0, 2075986, 0, 0,
-    0, 0, 0, 0, 0, 0, 1551218, 0,
-    0, 0, 0, 0, 0, 0, 0, 1485174,
+    1286998, 0, 0, 0, 0, 0, 0, 89,
+    0, 1220946, 0, 0, 0, 0, 93, 0,
+    0, 89, 1287002, 0, 0, 0, 0, 0,
+    93, 0, 0, 1220958, 0, 0, 0, 0,
+    0, 0, 0, 73, 1551174, 0, 0, 0,
+    0, 0, 77, 0, 0, 1485122, 0, 0,
+    0, 0, 0, 0, 0, 73, 1551178, 0,
+    0, 0, 0, 0, 77, 0, 0, 1485134,
 )
 KIND = (
     0, 1, 0, 1, 0, 1, 0, 0,
     1, 0, 1, 0, 1, 0, 0, 0,
-    0, 1, 0, 1, 0, 0, 0, 1,
-    1, 0, 1, 0, 0, 0, 1, 0,
+    0, 1, 0, 1, 0, 0, 1, 1,
+    1, 0, 1, 0, 0, 0, 1, 1,
     0, 1, 0, 0, 0, 1, 0, 1,
     1, 0, 0, 0, 1, 0, 1, 0,
-    0, 0, 0, 1, 0, 1, 0, 1,
-    0, 0, 1, 0, 1, 0, 1, 0,
+    0, 0, 1, 1, 0, 1, 0, 1,
+    0, 0, 1, 1, 1, 0, 1, 0,
 )
 
 F8 = jnp.float8_e4m3fn
 I32 = jnp.int32
 F32 = jnp.float32
 WORDS, ROWS, WIDE = 40, 640, 1280
-TALL = 640
-X, Y, Z = 4, 4, 4
 
 
 def look_up(table, d):
     return sum(jnp.where(d == i, I32(v), I32(0)) for i, v in enumerate(table) if v)
 
 
-def bit_set(row, mask):
-    return (jnp.broadcast_to(row, (32, row.shape[1])) & mask) != 0
-
-
-def ones(row, mask):
-    return jnp.where(bit_set(row, mask), 1.0, 0.0).astype(F8)
+def halves(words, top):
+    twice = jnp.concatenate([words, words], axis=0)
+    return jnp.where(top, twice & 0xFFFF, lax.shift_right_logical(twice, 16))
+
+
+def unpacked(words, top, bits):
+    part = halves(words, top)
+    part = jnp.concatenate([part, part], axis=0).astype(jnp.int16)
+    one, none = jnp.bfloat16(1), jnp.bfloat16(0)
+    rows = [jnp.where((part & b) != 0, one, none) for b in bits]
+    return [jnp.concatenate(rows[2 * j : 2 * j + 2], axis=0).astype(F8) for j in range(4)]
 
 
 def kernel(
     adj, rel, out, ratio_out,
-    own, inbox, w_rhs, w_lhs, acc, part_row, part_col, red_row, red_col, mine, every, want_ref,
+    plain, own, inbox, w_rhs, w_lhs, acc, part_row, part_col, red_row, red_col, mine, every, want_ref,
     adj_sem, send, relay_sem, in_sem, row_sem, col_sem, all_send, all_sem,
 ):
     row, col = lax.axis_index("row"), lax.axis_index("col")
     R, C, h = row // 2, col, row % 2
     g = 1 - h
     diag, off = R == C, R != C
-    fetch = pltpu.make_async_copy(adj, own, adj_sem)
+    fetch = pltpu.make_async_copy(adj, plain, adj_sem)
     fetch.start()
 
     barrier = pltpu.get_barrier_semaphore()
@@ -84,8 +87,17 @@
     lhs_is_own = diag | (kind == 1)
     rhs_is_own = kind == 0
 
-    mask = jnp.left_shift(I32(1), lax.broadcasted_iota(I32, (32, ROWS), 0))
+    p = lax.broadcasted_iota(I32, (8, 128), 1)
+    column = 32 * (p % 4) + 16 * (p // 4 % 2) + p // 8
     fetch.wait()
+
+    @pl.loop(0, 5)
+    def _(i):
+        at = pl.ds(pl.multiple_of(i * 8, 8), 8)
+        for k in range(5):
+            lanes = slice(k * 128, (k + 1) * 128)
+            own[at, lanes] = jnp.take_along_axis(plain[at, lanes], column, axis=1)
+
 
     @pl.when(lhs_is_own)
     def _():
@@ -109,11 +121,11 @@
         box = jnp.where(down == 1, 3 + 2 * slot + h, slot)
         r = jnp.where(down == 1, 2 * to + h, row)
         c = jnp.where(down == 1, col, to)
-        return code >= 64, copy(own, inbox.at[box], send.at[i], in_sem.at[box], r, c)
+        return code >= 64, slot, copy(own, inbox.at[box], send.at[i], in_sem.at[box], r, c)
 
     for i in range(7):
-        there, c = offer(i)
-        pl.when(there)(c.start)
+        there, slot, c = offer(i)
+        pl.when(there & (slot != 1))(c.start)
 
     def relay(s):
         box = 3 + 2 * s + h
@@ -130,26 +142,40 @@
         relay(s).start()
 
     first = jnp.where(diag, 2, 0)
+    acc[...] = jnp.zeros_like(acc)
     pass_on(first)
-    acc[...] = jnp.zeros_like(acc)
-
-    def unpack(box, to):
-        @pl.loop(0, 5)
-        def _(i):
-            base = pl.multiple_of(i * 8, 8)
-            for w in range(8):
-                to(
-                    pl.ds(pl.multiple_of(i * 256 + w * 32, 32), 32),
-                    ones(inbox[box, pl.ds(base + w, 1), :], mask),
-                )
-
-    def to_rhs(at, value):
-        w_rhs[at, :] = value
-
-    def to_lhs(k):
-        def put(at, value):
-            w_lhs[at, k * ROWS : (k + 1) * ROWS] = value
-        return put
+
+    for i in range(5):
+        there, slot, c = offer(i)
+        pl.when(there & (slot == 0))(c.wait_send)
+    for i in range(5):
+        there, slot, c = offer(i)
+        pl.when(there & (slot == 1))(c.start)
+
+    top = lax.broadcasted_iota(I32, (8, 128), 0) < 4
+    upper = lax.broadcasted_iota(I32, (16, 128), 0) < 8
+    bits = [
+        jnp.where(upper, I32(1 << k), I32(1 << (k + 1) if k < 14 else -32768)).astype(jnp.int16)
+        for k in range(0, 16, 2)
+    ]
+
+    def unpack(box, i, put):
+        for k in range(5):
+            words = inbox[box, pl.ds(pl.multiple_of(i * 8, 8), 8), k * 128 : (k + 1) * 128]
+            for q in range(2):
+                for j, piece in enumerate(unpacked(words[4 * q : 4 * q + 4], top, bits)):
+                    put(q * 128 + j * 32, k * 128, piece)
+
+    def product(lo, hi):
+        for k in range(2):
+            for i in range(lo, hi):
+                def put(r, c, piece):
+                    w_lhs[i * 256 + r : i * 256 + r + 32, k * ROWS + c : k * ROWS + c + 128] = piece
+                unpack(3 + 2 * s_now[0] + k, i, put)
+        at = slice(lo * 256, hi * 256)
+        acc[at, :] += jnp.dot(w_lhs[at, :], w_rhs[...], preferred_element_type=F32)
+
+    s_now = [None]
 
     @pl.loop(first, 3)
     def _(s):
@@ -157,49 +183,41 @@
         def _():
             arrived(s)
 
-        unpack(s, to_rhs)
+        @pl.loop(0, 5)
+        def _(i):
+            def put(r, c, piece):
+                w_rhs[pl.ds(pl.multiple_of(i * 256 + r, 32), 32), c : c + 128] = piece
+            unpack(s, i, put)
+
+        arrived(3 + 2 * s + g)
+        s_now[0] = s
+        product(0, 3)
 
         @pl.when(s < 2)
         def _():
             pass_on(s + 1)
 
-        def half(k):
-            @pl.when(k == g)
-            def _():
-                arrived(3 + 2 * s + k)
-
-            unpack(3 + 2 * s + k, to_lhs(k))
-
-        half(0)
-        half(1)
-
-        @pl.loop(0, WIDE // TALL)
-        def _(i):
-            at = pl.ds(pl.multiple_of(i * TALL, TALL), TALL)
-            acc[at, :] += jnp.dot(w_lhs[at, :], w_rhs[...], preferred_element_type=F32)
-
-    def fold(i, carry):
-        closed, degree = carry
-        base = pl.multiple_of(i * 8, 8)
+        product(3, 5)
+
+    def fold(i, closed):
+        words = own[pl.ds(pl.multiple_of(i * 8, 8), 8), :]
         for q in range(2):
+            part = halves(words[4 * q : 4 * q + 4], wide_top)
             sums = []
-            for w in range(4):
-                at = pl.multiple_of(i * 256 + q * 128 + w * 32, 32)
-                bit = bit_set(own[pl.ds(base + q * 4 + w, 1), :], mask)
-                val = jnp.where(bit, acc[pl.ds(at, 32), :], 0.0)
-                one = jnp.where(bit, 1.0, 0.0)
-                closed = closed + jnp.sum(val.reshape(4, 8, ROWS), axis=0)
-                degree = degree + jnp.sum(one.reshape(4, 8, ROWS), axis=0)
+            for k in range(16):
+                at = pl.multiple_of(i * 256 + q * 128 + k * 8, 8)
+                val = jnp.where((part & (1 << k)) != 0, acc[pl.ds(at, 8), :], 0.0)
+                closed = closed + val
                 sums.append(sum(val[:, k * 128 : (k + 1) * 128] for k in range(5)))
             across = jnp.concatenate(sums, axis=0).T
             part_col[2 * i + q, :, :] = jnp.sum(across, axis=0, keepdims=True)
-        return closed, degree
-
-    zeros = jnp.zeros((8, ROWS), F32)
-    closed, degree = lax.fori_loop(0, 5, fold, (zeros, zeros))
+        return closed
+
+    wide_top = lax.broadcasted_iota(I32, (8, ROWS), 0) < 4
+    degree = jnp.sum(lax.population_count(own[...]), axis=0, keepdims=True).astype(F32)
+    closed = lax.fori_loop(0, 5, fold, jnp.zeros((8, ROWS), F32))
     once_more = kind.astype(F32)
     closed = jnp.sum(closed, axis=0, keepdims=True) * (1.0 + once_more)
-    degree = jnp.sum(degree, axis=0, keepdims=True)
     part_col[...] = part_col[...] * (2.0 - once_more)
     for k in range(5):
         part_row[k, :, :] = closed[:, k * 128 : (k + 1) * 128]
@@ -220,23 +238,19 @@
         for c in give_col:
             c.start()
 
-    def tell(dx, i, k):
-        x, y, z = C // 4 * 2 + R % 2, R // 2, C % 4
-        x, y, z = (x + dx) % X, (y + 2 + i // 4) % Y, (z + 2 + i % 4) % Z
-        r, c = y * 4 + x % 2 * 2 + k, x // 2 * 4 + z
+    def tell(r, c):
         return copy(mine, every.at[row], all_send.at[r * 8 + c], all_sem.at[row], r, c)
 
-    HOME = 10
-
     def for_all(act):
-        for dx in (2, 1, 3, 0):
-            @pl.loop(0, 16)
-            def _(i):
-                @pl.when((i != HOME) | (dx != 0))
-                def _():
-                    for k in range(2):
-                        act(tell(dx, i, k))
-        act(tell(0, HOME, g))
+        for x in (0, 1, 3, 2):
+            for y in (0, 1, 3, 2):
+                @pl.loop(0, 8)
+                def _(i):
+                    r, c = y * 4 + x % 2 * 2 + i % 2, x // 2 * 4 + i // 2
+
+                    @pl.when((r != row) | (c != col))
+                    def _():
+                        act(tell(r, c))
 
     @pl.when(diag)
     def _():
@@ -273,11 +287,12 @@
     want = jnp.broadcast_to(want_ref[...], (6, 128))
     block, rest = want // ROWS, want % ROWS
     line, lane = rest // 128, rest % 128
+    lane = 8 * (lane % 16) + 4 * (lane // 16 % 2) + lane // 32
     here = lax.broadcasted_iota(I32, (6, 128), 0) == line
 
     for i in range(7):
-        there, c = offer(i)
-        pl.when(there)(c.wait_send)
+        there, slot, c = offer(i)
+        pl.when(there & (slot != 0))(c.wait_send)
 
     @pl.loop(first, 3)
     def _(s):
@@ -320,6 +335,7 @@
         in_specs=[pl.BlockSpec(memory_space=pl.ANY), pl.BlockSpec(memory_space=vmem)],
         out_specs=[pl.BlockSpec(memory_space=vmem)] * 2,
         scratch_shapes=[
+            vmem((WORDS, ROWS), I32),
             vmem((WORDS, ROWS), I32),
             vmem((9, WORDS, ROWS), I32),
             vmem((WIDE, ROWS), F8),
@@ -342,7 +358,7 @@
             dma((16,)),
         ],
         compiler_params=pltpu.CompilerParams(
-            collective_id=0, has_side_effects=True, vmem_limit_bytes=48 * 2**20
+            collective_id=0, has_side_effects=True, vmem_limit_bytes=67043328
         ),
     )(adjacency.T, relabel[None, :])
     return out[0], ratio[0, 0]

time: 48.8 us -> 44.3 us (0.908)
  Pallas kernels: 44.2 us -> 40.3 us
  local copies, waits for them, and re-layouts: 2.06 us -> 1.13 us
    pallas_call x1, Pallas kernels: 44.2 us -> 40.3 us  [body(): pl.pallas_call(kernel, out_shape=(jax.ShapeDtypeStruct((1, 80), F32), jax...]
    unnamed x5 -> x3, local copies, waits for them, and re-layouts: 2.06 us -> 1.13 us
where the time goes in v3:
time: 44.3 us; the launch traced here: 43.8 us
  Pallas kernels  40.3 us (91%)
  between operations  2.41 us (5%)
  local copies, waits for them, and re-layouts  1.13 us (3%)
    pallas_call x1, Pallas kernels, body(): pl.pallas_call(kernel, out_shape=(jax.ShapeDtypeStruct((1, 80), F32), jax...  40.3 us
    unnamed x3, local copies, waits for them, and re-layouts  1.13 us

profile of v3, /device:TPU:1, one launch (start us, length us, event | category | flops | bytes accessed | tf_op | source)
XLA Modules:
  0.0 43.8 jit_solution(14078728164805417576)
XLA Ops:
  0.6 40.3 %shard_map.41 = (f32[1,80]{1,0:T(1,128)}, f32[1,1]{1,0:T(1,128)}) custom-call(s32[40,640]{1,0:T(8,128)} %bitcast.4, s32[1,80]{1,0:T(1,128)} %bitcast.5), custom_call_target="tpu_custom_call" | custom-call | tf_op jit(solution)/shard_map/pallas_call | solution.py:332
  40.9 0.0 copy-start
  40.9 0.6 %copy-done = f32[1,80]{1,0:T(1,128)S(1)} copy-done((f32[1,80]{1,0:T(1,128)S(1)}, f32[1,80]{1,0:T(1,128)}, u32[]{:S(2)}) %copy-start) | copy-done | bytes 344
  41.6 0.5 %copy.6 = f32[80]{0:T(128)} copy(f32[80]{0:T(128)S(1)} %bitcast.6) | data formatting | bytes 640
Async XLA Ops:
  40.9 0.6 %copy-start = (f32[1,80]{1,0:T(1,128)S(1)}, f32[1,80]{1,0:T(1,128)}, u32[]{:S(2)}) copy-start(f32[1,80]{1,0:T(1,128)} %get-tuple-element.4) | copy-start | bytes 964

commit v4 on v3

--- a/solution.py
+++ b/solution.py
@@ -121,11 +121,11 @@
         box = jnp.where(down == 1, 3 + 2 * slot + h, slot)
         r = jnp.where(down == 1, 2 * to + h, row)
         c = jnp.where(down == 1, col, to)
-        return code >= 64, slot, copy(own, inbox.at[box], send.at[i], in_sem.at[box], r, c)
+        return code >= 64, copy(own, inbox.at[box], send.at[i], in_sem.at[box], r, c)
 
     for i in range(7):
-        there, slot, c = offer(i)
-        pl.when(there & (slot != 1))(c.start)
+        there, c = offer(i)
+        pl.when(there)(c.start)
 
     def relay(s):
         box = 3 + 2 * s + h
@@ -144,13 +144,6 @@
     first = jnp.where(diag, 2, 0)
     acc[...] = jnp.zeros_like(acc)
     pass_on(first)
-
-    for i in range(5):
-        there, slot, c = offer(i)
-        pl.when(there & (slot == 0))(c.wait_send)
-    for i in range(5):
-        there, slot, c = offer(i)
-        pl.when(there & (slot == 1))(c.start)
 
     top = lax.broadcasted_iota(I32, (8, 128), 0) < 4
     upper = lax.broadcasted_iota(I32, (16, 128), 0) < 8
@@ -223,30 +216,32 @@
         part_row[k, :, :] = closed[:, k * 128 : (k + 1) * 128]
         part_row[5 + k, :, :] = degree[:, k * 128 : (k + 1) * 128]
 
-    give_row = copy(part_row, red_row.at[C], send.at[7], row_sem.at[C], row, R)
-    give_col = [
-        copy(
-            part_col.at[pl.ds(5 * k, 5)], red_col.at[R, h], send.at[8 + k],
-            col_sem.at[R, h], 2 * C + k, C,
-        )
+    give_row = [
+        copy(part_row, red_row.at[C, h], send.at[7 + k], row_sem.at[C, h], 2 * R + k, R)
         for k in range(2)
     ]
+    give_col = [
+        copy(part_col, red_col.at[R, h], send.at[9 + k], col_sem.at[R, h], 2 * C + k, C)
+        for k in range(2)
+    ]
 
     @pl.when(off)
     def _():
-        give_row.start()
-        for c in give_col:
+        for c in give_row + give_col:
             c.start()
 
+    to_other = copy(part_row, red_row.at[C, h], send.at[7], row_sem.at[C, h], 2 * R + g, C)
+    pl.when(diag)(to_other.start)
+
     def tell(r, c):
-        return copy(mine, every.at[row], all_send.at[r * 8 + c], all_sem.at[row], r, c)
+        return copy(mine, every.at[R], all_send.at[r // 2 * 8 + c], all_sem.at[R], r, c)
 
     def for_all(act):
         for x in (0, 1, 3, 2):
             for y in (0, 1, 3, 2):
-                @pl.loop(0, 8)
+                @pl.loop(0, 4)
                 def _(i):
-                    r, c = y * 4 + x % 2 * 2 + i % 2, x // 2 * 4 + i // 2
+                    r, c = y * 4 + x % 2 * 2 + h, x // 2 * 4 + i
 
                     @pl.when((r != row) | (c != col))
                     def _():
@@ -254,45 +249,53 @@
 
     @pl.when(diag)
     def _():
-        tot = part_row[...]
-
-        def add(i, tot):
+        copy(part_row, red_row.at[C, g], send.at[0], row_sem.at[C, g], row, col).wait_recv()
+        red_row[C, h] = part_row[...]
+        flat = jnp.zeros((10, 1, 128), F32)
+
+        def add(i, carry):
+            closed, degree, across = carry
             o = (R + i) % 8
-            copy(part_row, red_row.at[o], send.at[0], row_sem.at[o], row, col).wait_recv()
-            tot = tot + red_row[o]
-            both = jnp.zeros((5, 1, 128), F32)
             for k in range(2):
                 copy(
-                    part_col.at[pl.ds(0, 5)], red_col.at[o, k], send.at[0],
-                    col_sem.at[o, k], row, col,
+                    part_row, red_row.at[o, k], send.at[0], row_sem.at[o, k], row, col
                 ).wait_recv()
-                both = both + red_col[o, k]
-            return tot + jnp.concatenate([both, jnp.zeros_like(both)], axis=0)
-
-        tot = lax.fori_loop(1, 8, add, tot)
-        total, deg = tot[:5, 0, :], tot[5:, 0, :]
+                copy(
+                    part_col, red_col.at[o, k], send.at[0], col_sem.at[o, k], row, col
+                ).wait_recv()
+                across = across + red_col[o, k]
+            sums = [red_row[o, k] for k in range(2)]
+            closed = closed + jnp.concatenate([v[:5] for v in sums], axis=0)
+            degree = degree + jnp.concatenate([v[5:] for v in sums], axis=0)
+            return closed, degree, across
+
+        sums = [red_row[C, k] for k in range(2)]
+        closed = jnp.concatenate([v[:5] for v in sums], axis=0)
+        degree = jnp.concatenate([v[5:] for v in sums], axis=0)
+        closed, degree, across = lax.fori_loop(1, 8, add, (closed, degree, flat))
+        total, deg = (closed + across)[:, 0, :], degree[:, 0, :]
         wedges = jnp.maximum(deg * (deg - 1.0), 1.0)
-        mine[0:5, :] = total / wedges
+        mine[0:10, :] = total / wedges
         low = lax.broadcasted_iota(I32, (1, 128), 1) < 64
         both = []
         for v in (total, wedges):
             v = jnp.sum(v, axis=0, keepdims=True)
             both.append(v + pltpu.roll(v, 64, 1))
-        mine[5:6, :] = jnp.where(low, both[0], both[1])
-        every[row] = mine[...]
+        mine[10:11, :] = jnp.where(low, both[0], both[1])
+        every[C] = mine[...]
         for_all(lambda c: c.start())
 
     want_ref[...] = jnp.zeros_like(want_ref)
     want_ref[:, 0:80] = rel[...]
-    want = jnp.broadcast_to(want_ref[...], (6, 128))
-    block, rest = want // ROWS, want % ROWS
+    want = jnp.broadcast_to(want_ref[...], (11, 128))
+    block, rest = want // WIDE, want % WIDE
     line, lane = rest // 128, rest % 128
     lane = 8 * (lane % 16) + 4 * (lane // 16 % 2) + lane // 32
-    here = lax.broadcasted_iota(I32, (6, 128), 0) == line
+    here = lax.broadcasted_iota(I32, (11, 128), 0) == line
 
     for i in range(7):
-        there, slot, c = offer(i)
-        pl.when(there & (slot != 0))(c.wait_send)
+        there, c = offer(i)
+        pl.when(there)(c.wait_send)
 
     @pl.loop(first, 3)
     def _(s):
@@ -300,19 +303,20 @@
 
     @pl.when(off)
     def _():
-        give_row.wait_send()
-        for c in give_col:
+        for c in give_row + give_col:
             c.wait_send()
 
-    found = jnp.zeros((6, 128), F32)
+    pl.when(diag)(to_other.wait_send)
+
+    found = jnp.zeros((11, 128), F32)
     sums = jnp.zeros((1, 128), F32)
-    for b in range(16):
-        @pl.when(off | (row != b))
+    for b in range(8):
+        @pl.when(off | (R != b))
         def _():
             copy(mine, every.at[b], all_send.at[0], all_sem.at[b], row, col).wait_recv()
 
         tile = every[b]
-        sums = sums + tile[5:6, :]
+        sums = sums + tile[10:11, :]
         got = jnp.take_along_axis(tile, lane, axis=1)
         found = found + jnp.where(here & (block == b), got, 0.0)
     low = lax.broadcasted_iota(I32, (1, 128), 1) < 64
@@ -343,19 +347,19 @@
             vmem((WIDE, ROWS), F32),
             vmem((10, 1, 128), F32),
             vmem((10, 1, 128), F32),
-            vmem((8, 10, 1, 128), F32),
-            vmem((8, 2, 5, 1, 128), F32),
-            vmem((6, 128), F32),
-            vmem((16, 6, 128), F32),
+            vmem((8, 2, 10, 1, 128), F32),
+            vmem((8, 2, 10, 1, 128), F32),
+            vmem((11, 128), F32),
+            vmem((8, 11, 128), F32),
             vmem((1, 128), I32),
             dma,
-            dma((10,)),
+            dma((11,)),
             dma((3,)),
             dma((9,)),
+            dma((8, 2)),
+            dma((8, 2)),
+            dma((64,)),
             dma((8,)),
-            dma((8, 2)),
-            dma((128,)),
-            dma((16,)),
         ],
         compiler_params=pltpu.CompilerParams(
             collective_id=0, has_side_effects=True, vmem_limit_bytes=67043328

time: 44.3 us -> 40.2 us (0.907)
  Pallas kernels: 40.3 us -> 36.3 us
    pallas_call x1, Pallas kernels: 40.3 us -> 36.3 us  [body(): pl.pallas_call(kernel, out_shape=(jax.ShapeDtypeStruct((1, 80), F32), jax...]
where the time goes in v4:
time: 40.2 us; the launch traced here: 39.9 us
  Pallas kernels  36.3 us (90%)
  between operations  2.41 us (6%)
  local copies, waits for them, and re-layouts  1.13 us (3%)
    pallas_call x1, Pallas kernels, body(): pl.pallas_call(kernel, out_shape=(jax.ShapeDtypeStruct((1, 80), F32), jax...  36.3 us
    unnamed x3, local copies, waits for them, and re-layouts  1.13 us

profile of v4, /device:TPU:1, one launch (start us, length us, event | category | flops | bytes accessed | tf_op | source)
XLA Modules:
  0.0 39.9 jit_solution(5617548034630913213)
XLA Ops:
  0.6 36.3 %shard_map.41 = (f32[1,80]{1,0:T(1,128)}, f32[1,1]{1,0:T(1,128)}) custom-call(s32[40,640]{1,0:T(8,128)} %bitcast.4, s32[1,80]{1,0:T(1,128)} %bitcast.5), custom_call_target="tpu_custom_call" | custom-call | tf_op jit(solution)/shard_map/pallas_call | solution.py:336
  37.0 0.0 copy-start
  37.0 0.6 %copy-done = f32[1,80]{1,0:T(1,128)S(1)} copy-done((f32[1,80]{1,0:T(1,128)S(1)}, f32[1,80]{1,0:T(1,128)}, u32[]{:S(2)}) %copy-start) | copy-done | bytes 344
  37.6 0.5 %copy.6 = f32[80]{0:T(128)} copy(f32[80]{0:T(128)S(1)} %bitcast.6) | data formatting | bytes 640
Async XLA Ops:
  37.0 0.6 %copy-start = (f32[1,80]{1,0:T(1,128)S(1)}, f32[1,80]{1,0:T(1,128)}, u32[]{:S(2)}) copy-start(f32[1,80]{1,0:T(1,128)} %get-tuple-element.4) | copy-start | bytes 964

commit v5 on v4

--- a/solution.py
+++ b/solution.py
@@ -6,34 +6,34 @@
 from jax.sharding import PartitionSpec as P
 
 SENDS_A = (
-    257605490, 171605116, 163537496, 1866856, 197031157, 146367608, 179465804, 229911156,
-    180303480, 266059126, 1801844, 155082844, 138375372, 230452348, 221587568, 187983560,
-    146040436, 238973044, 199012726, 205355132, 137833028, 1539792, 180121724, 162930800,
-    247427696, 154493040, 247036152, 190690162, 1469048, 137766980, 146220148, 171801828,
-    163476709, 180186216, 146171484, 263201380, 257603426, 138310764, 196831816, 1604712,
-    171734748, 263742572, 254877792, 154169048, 146749032, 266057062, 2061924, 188377164,
-    171123284, 1275584, 146307180, 196225120, 179334756, 205158500, 165458278, 238645356,
-    1204840, 171057236, 179514468, 137983220, 213613152, 187787360, 247034088, 157135714,
+    257605490, 171736168, 196289112, 247346300, 180321384, 187856101, 146221640, 163478224,
+    180190828, 266059126, 239023736, 187834460, 196833529, 171867756, 154369748, 137766988,
+    179511888, 263991412, 240696694, 196507744, 162998848, 146570968, 230520928, 170948321,
+    255668848, 171057236, 188185188, 249151346, 137460444, 154544196, 179991281, 222067300,
+    146504808, 155089645, 179511896, 196506816, 257603426, 137919592, 162998856, 213791852,
+    163020529, 138051180, 188444868, 171057244, 146374252, 266057062, 205469288, 154544204,
+    196289104, 179597512, 263813216, 138377445, 146221632, 230436964, 240694630, 162691168,
+    171537612, 187834452, 146111733, 255359588, 222114400, 137766980, 154368612, 249149282,
 )
 SENDS_B = (
-    1286998, 0, 0, 0, 0, 0, 0, 89,
-    0, 1220946, 0, 0, 0, 0, 93, 0,
-    0, 89, 1287002, 0, 0, 0, 0, 0,
-    93, 0, 0, 1220958, 0, 0, 0, 0,
-    0, 0, 0, 73, 1551174, 0, 0, 0,
-    0, 0, 77, 0, 0, 1485122, 0, 0,
-    0, 0, 0, 0, 0, 73, 1551178, 0,
-    0, 0, 0, 0, 77, 0, 0, 1485134,
+    1286998, 0, 0, 0, 0, 0, 0, 0,
+    0, 1220946, 0, 0, 0, 0, 0, 0,
+    0, 0, 1287006, 0, 0, 0, 0, 0,
+    0, 0, 0, 1220954, 0, 0, 0, 0,
+    0, 0, 0, 0, 1551174, 0, 0, 0,
+    0, 0, 0, 0, 0, 1485122, 0, 0,
+    0, 0, 0, 0, 0, 0, 1551182, 0,
+    0, 0, 0, 0, 0, 0, 0, 1485130,
 )
 KIND = (
-    0, 1, 0, 1, 0, 1, 0, 0,
-    1, 0, 1, 0, 1, 0, 0, 0,
-    0, 1, 0, 1, 0, 0, 1, 1,
-    1, 0, 1, 0, 0, 0, 1, 1,
-    0, 1, 0, 0, 0, 1, 0, 1,
-    1, 0, 0, 0, 1, 0, 1, 0,
-    0, 0, 1, 1, 0, 1, 0, 1,
-    0, 0, 1, 1, 1, 0, 1, 0,
+    0, 7, 2, 7, 3, 4, 0, 1,
+    7, 0, 7, 0, 4, 3, 1, 0,
+    2, 7, 0, 7, 0, 1, 3, 6,
+    7, 0, 7, 0, 1, 0, 6, 3,
+    3, 4, 0, 1, 0, 7, 0, 7,
+    4, 3, 1, 0, 7, 0, 7, 2,
+    0, 1, 3, 6, 0, 7, 0, 7,
+    1, 0, 6, 3, 7, 2, 7, 0,
 )
 
 F8 = jnp.float8_e4m3fn
@@ -82,7 +82,8 @@
     hello(2 * R + g, C)
 
     place = R * 8 + C
-    kind = look_up(KIND, place)
+    kinds = look_up(KIND, place)
+    kind = kinds // 4
     codes_a, codes_b = look_up(SENDS_A, place), look_up(SENDS_B, place)
     lhs_is_own = diag | (kind == 1)
     rhs_is_own = kind == 0
@@ -142,7 +143,8 @@
         relay(s).start()
 
     first = jnp.where(diag, 2, 0)
-    acc[...] = jnp.zeros_like(acc)
+    for k in range(2):
+        acc[k] = jnp.zeros_like(acc[k])
     pass_on(first)
 
     top = lax.broadcasted_iota(I32, (8, 128), 0) < 4
@@ -166,9 +168,9 @@
                     w_lhs[i * 256 + r : i * 256 + r + 32, k * ROWS + c : k * ROWS + c + 128] = piece
                 unpack(3 + 2 * s_now[0] + k, i, put)
         at = slice(lo * 256, hi * 256)
-        acc[at, :] += jnp.dot(w_lhs[at, :], w_rhs[...], preferred_element_type=F32)
-
-    s_now = [None]
+        acc[t_now[0], at, :] += jnp.dot(w_lhs[at, :], w_rhs[...], preferred_element_type=F32)
+
+    s_now, t_now = [None], [None]
 
     @pl.loop(first, 3)
     def _(s):
@@ -184,6 +186,7 @@
 
         arrived(3 + 2 * s + g)
         s_now[0] = s
+        t_now[0] = jnp.where(s == 0, kinds % 2, jnp.where(s == 1, kinds // 2 % 2, kind))
         product(0, 3)
 
         @pl.when(s < 2)
@@ -194,24 +197,28 @@
 
     def fold(i, closed):
         words = own[pl.ds(pl.multiple_of(i * 8, 8), 8), :]
+        once, twice = closed
         for q in range(2):
             part = halves(words[4 * q : 4 * q + 4], wide_top)
             sums = []
             for k in range(16):
-                at = pl.multiple_of(i * 256 + q * 128 + k * 8, 8)
-                val = jnp.where((part & (1 << k)) != 0, acc[pl.ds(at, 8), :], 0.0)
-                closed = closed + val
-                sums.append(sum(val[:, k * 128 : (k + 1) * 128] for k in range(5)))
+                at = pl.ds(pl.multiple_of(i * 256 + q * 128 + k * 8, 8), 8)
+                bit = (part & (1 << k)) != 0
+                a = jnp.where(bit, acc[0, at, :], 0.0)
+                b = jnp.where(bit, acc[1, at, :], 0.0)
+                once, twice = once + a, twice + b
+                a = sum(a[:, k * 128 : (k + 1) * 128] for k in range(5))
+                b = sum(b[:, k * 128 : (k + 1) * 128] for k in range(5))
+                sums.append(2.0 * a + b)
             across = jnp.concatenate(sums, axis=0).T
             part_col[2 * i + q, :, :] = jnp.sum(across, axis=0, keepdims=True)
-        return closed
+        return once, twice
 
     wide_top = lax.broadcasted_iota(I32, (8, ROWS), 0) < 4
     degree = jnp.sum(lax.population_count(own[...]), axis=0, keepdims=True).astype(F32)
-    closed = lax.fori_loop(0, 5, fold, jnp.zeros((8, ROWS), F32))
-    once_more = kind.astype(F32)
-    closed = jnp.sum(closed, axis=0, keepdims=True) * (1.0 + once_more)
-    part_col[...] = part_col[...] * (2.0 - once_more)
+    zeros = jnp.zeros((8, ROWS), F32)
+    once, twice = lax.fori_loop(0, 5, fold, (zeros, zeros))
+    closed = jnp.sum(once + 2.0 * twice, axis=0, keepdims=True)
     for k in range(5):
         part_row[k, :, :] = closed[:, k * 128 : (k + 1) * 128]
         part_row[5 + k, :, :] = degree[:, k * 128 : (k + 1) * 128]
@@ -237,15 +244,14 @@
         return copy(mine, every.at[R], all_send.at[r // 2 * 8 + c], all_sem.at[R], r, c)
 
     def for_all(act):
-        for x in (0, 1, 3, 2):
-            for y in (0, 1, 3, 2):
-                @pl.loop(0, 4)
-                def _(i):
-                    r, c = y * 4 + x % 2 * 2 + h, x // 2 * 4 + i
-
-                    @pl.when((r != row) | (c != col))
-                    def _():
-                        act(tell(r, c))
+        where = [(x, y, z) for x in range(4) for y in range(4) for z in range(4)]
+        where.sort(key=lambda v: sum(min(a, 4 - a) for a in v))
+        for x, y, z in where:
+            r, c = y * 4 + x % 2 * 2 + h, x // 2 * 4 + z
+
+            @pl.when((r != row) | (c != col))
+            def _():
+                act(tell(r, c))
 
     @pl.when(diag)
     def _():
@@ -344,7 +350,7 @@
             vmem((9, WORDS, ROWS), I32),
             vmem((WIDE, ROWS), F8),
             vmem((WIDE, WIDE), F8),
-            vmem((WIDE, ROWS), F32),
+            vmem((2, WIDE, ROWS), F32),
             vmem((10, 1, 128), F32),
             vmem((10, 1, 128), F32),
             vmem((8, 2, 10, 1, 128), F32),

time: 40.2 us -> 38.1 us (0.948)
  Pallas kernels: 36.3 us -> 34.3 us
    pallas_call x1, Pallas kernels: 36.3 us -> 34.3 us  [body(): pl.pallas_call(kernel, out_shape=(jax.ShapeDtypeStruct((1, 80), F32), jax...]
where the time goes in v5:
time: 38.1 us; the launch traced here: 37.9 us
  Pallas kernels  34.3 us (90%)
  between operations  2.41 us (6%)
  local copies, waits for them, and re-layouts  1.13 us (3%)
    pallas_call x1, Pallas kernels, body(): pl.pallas_call(kernel, out_shape=(jax.ShapeDtypeStruct((1, 80), F32), jax...  34.3 us
    unnamed x3, local copies, waits for them, and re-layouts  1.13 us

profile of v5, /device:TPU:1, one launch (start us, length us, event | category | flops | bytes accessed | tf_op | source)
XLA Modules:
  0.0 37.9 jit_solution(2412318291324980943)
XLA Ops:
  0.6 34.3 %shard_map.41 = (f32[1,80]{1,0:T(1,128)}, f32[1,1]{1,0:T(1,128)}) custom-call(s32[40,640]{1,0:T(8,128)} %bitcast.4, s32[1,80]{1,0:T(1,128)} %bitcast.5), custom_call_target="tpu_custom_call" | custom-call | tf_op jit(solution)/shard_map/pallas_call | solution.py:342
  35.0 0.0 copy-start
  35.0 0.6 %copy-done = f32[1,80]{1,0:T(1,128)S(1)} copy-done((f32[1,80]{1,0:T(1,128)S(1)}, f32[1,80]{1,0:T(1,128)}, u32[]{:S(2)}) %copy-start) | copy-done | bytes 344
  35.6 0.5 %copy.6 = f32[80]{0:T(128)} copy(f32[80]{0:T(128)S(1)} %bitcast.6) | data formatting | bytes 640
Async XLA Ops:
  35.0 0.6 %copy-start = (f32[1,80]{1,0:T(1,128)S(1)}, f32[1,80]{1,0:T(1,128)}, u32[]{:S(2)}) copy-start(f32[1,80]{1,0:T(1,128)} %get-tuple-element.4) | copy-start | bytes 964

commit v6 on v5

--- a/solution.py
+++ b/solution.py
@@ -61,8 +61,8 @@
 
 def kernel(
     adj, rel, out, ratio_out,
-    plain, own, inbox, w_rhs, w_lhs, acc, part_row, part_col, red_row, red_col, mine, every, want_ref,
-    adj_sem, send, relay_sem, in_sem, row_sem, col_sem, all_send, all_sem,
+    plain, own, inbox, w_rhs, w_lhs, acc, part_row, part_col, red_row, red_col, mine, every, rel_here, want_ref,
+    adj_sem, rel_sem, send, relay_sem, in_sem, row_sem, col_sem, all_send, all_sem,
 ):
     row, col = lax.axis_index("row"), lax.axis_index("col")
     R, C, h = row // 2, col, row % 2
@@ -70,6 +70,8 @@
     diag, off = R == C, R != C
     fetch = pltpu.make_async_copy(adj, plain, adj_sem)
     fetch.start()
+    fetch_rel = pltpu.make_async_copy(rel, rel_here, rel_sem)
+    fetch_rel.start()
 
     barrier = pltpu.get_barrier_semaphore()
 
@@ -292,7 +294,8 @@
         for_all(lambda c: c.start())
 
     want_ref[...] = jnp.zeros_like(want_ref)
-    want_ref[:, 0:80] = rel[...]
+    fetch_rel.wait()
+    want_ref[:, 0:80] = rel_here[...]
     want = jnp.broadcast_to(want_ref[...], (11, 128))
     block, rest = want // WIDE, want % WIDE
     line, lane = rest // 128, rest % 128
@@ -342,7 +345,7 @@
     out, ratio = pl.pallas_call(
         kernel,
         out_shape=(jax.ShapeDtypeStruct((1, 80), F32), jax.ShapeDtypeStruct((1, 1), F32)),
-        in_specs=[pl.BlockSpec(memory_space=pl.ANY), pl.BlockSpec(memory_space=vmem)],
+        in_specs=[pl.BlockSpec(memory_space=pl.ANY)] * 2,
         out_specs=[pl.BlockSpec(memory_space=vmem)] * 2,
         scratch_shapes=[
             vmem((WORDS, ROWS), I32),
@@ -357,7 +360,9 @@
             vmem((8, 2, 10, 1, 128), F32),
             vmem((11, 128), F32),
             vmem((8, 11, 128), F32),
+            vmem((1, 80), I32),
             vmem((1, 128), I32),
+            dma,
             dma,
             dma((11,)),
             dma((3,)),

time: 38.1 us -> 37.4 us (0.982)
  Pallas kernels: 34.3 us -> 33.7 us
    pallas_call x1, Pallas kernels: 34.3 us -> 33.7 us  [body(): pl.pallas_call(kernel, out_shape=(jax.ShapeDtypeStruct((1, 80), F32), jax...]
where the time goes in v6:
time: 37.4 us; the launch traced here: 37.3 us
  Pallas kernels  33.7 us (90%)
  between operations  2.41 us (6%)
  local copies, waits for them, and re-layouts  1.13 us (3%)
    pallas_call x1, Pallas kernels, body(): pl.pallas_call(kernel, out_shape=(jax.ShapeDtypeStruct((1, 80), F32), jax...  33.7 us
    unnamed x3, local copies, waits for them, and re-layouts  1.13 us

profile of v6, /device:TPU:1, one launch (start us, length us, event | category | flops | bytes accessed | tf_op | source)
XLA Modules:
  0.0 37.3 jit_solution(17651390359032981642)
XLA Ops:
  0.6 33.7 %shard_map.41 = (f32[1,80]{1,0:T(1,128)}, f32[1,1]{1,0:T(1,128)}) custom-call(s32[40,640]{1,0:T(8,128)} %bitcast.4, s32[1,80]{1,0:T(1,128)} %bitcast.5), custom_call_target="tpu_custom_call" | custom-call | tf_op jit(solution)/shard_map/pallas_call | solution.py:345
  34.4 0.0 copy-start
  34.4 0.6 %copy-done = f32[1,80]{1,0:T(1,128)S(1)} copy-done((f32[1,80]{1,0:T(1,128)S(1)}, f32[1,80]{1,0:T(1,128)}, u32[]{:S(2)}) %copy-start) | copy-done | bytes 344
  35.0 0.5 %copy.6 = f32[80]{0:T(128)} copy(f32[80]{0:T(128)S(1)} %bitcast.6) | data formatting | bytes 640
Async XLA Ops:
  34.4 0.6 %copy-start = (f32[1,80]{1,0:T(1,128)S(1)}, f32[1,80]{1,0:T(1,128)}, u32[]{:S(2)}) copy-start(f32[1,80]{1,0:T(1,128)} %get-tuple-element.4) | copy-start | bytes 964

commit v7 on v6

--- a/solution.py
+++ b/solution.py
@@ -61,7 +61,7 @@
 
 def kernel(
     adj, rel, out, ratio_out,
-    plain, own, inbox, w_rhs, w_lhs, acc, part_row, part_col, red_row, red_col, mine, every, rel_here, want_ref,
+    plain, own, inbox, w_rhs, w_lhs, part_row, part_col, red_row, red_col, mine, every, rel_here, want_ref,
     adj_sem, rel_sem, send, relay_sem, in_sem, row_sem, col_sem, all_send, all_sem,
 ):
     row, col = lax.axis_index("row"), lax.axis_index("col")
@@ -144,10 +144,13 @@
 
         relay(s).start()
 
-    first = jnp.where(diag, 2, 0)
-    for k in range(2):
-        acc[k] = jnp.zeros_like(acc[k])
-    pass_on(first)
+    last = jnp.where(diag, 1, 3)
+    degree = jnp.sum(lax.population_count(own[...]), axis=0, keepdims=True).astype(F32)
+    part_row[...] = jnp.zeros_like(part_row)
+    part_col[...] = jnp.zeros_like(part_col)
+    for k in range(5):
+        part_row[5 + k, :, :] = degree[:, k * 128 : (k + 1) * 128]
+    pass_on(2)
 
     top = lax.broadcasted_iota(I32, (8, 128), 0) < 4
     upper = lax.broadcasted_iota(I32, (16, 128), 0) < 8
@@ -170,12 +173,30 @@
                     w_lhs[i * 256 + r : i * 256 + r + 32, k * ROWS + c : k * ROWS + c + 128] = piece
                 unpack(3 + 2 * s_now[0] + k, i, put)
         at = slice(lo * 256, hi * 256)
-        acc[t_now[0], at, :] += jnp.dot(w_lhs[at, :], w_rhs[...], preferred_element_type=F32)
-
+        paths = jnp.dot(w_lhs[at, :], w_rhs[...], preferred_element_type=F32)
+        closed = jnp.zeros((8, ROWS), F32)
+        for n in range(2 * (hi - lo)):
+            words = own[(2 * lo + n) * 4 : (2 * lo + n) * 4 + 4, :]
+            part = halves(words, wide_top)
+            sums = []
+            for k in range(16):
+                r = n * 128 + k * 8
+                val = jnp.where((part & (1 << k)) != 0, paths[r : r + 8, :], 0.0)
+                closed = closed + val
+                sums.append(sum(val[:, j * 128 : (j + 1) * 128] for j in range(5)))
+            across = jnp.sum(jnp.concatenate(sums, axis=0).T, axis=0, keepdims=True)
+            part_col[2 * lo + n, :, :] += across * (2.0 - t_now[0])
+        closed = jnp.sum(closed, axis=0, keepdims=True) * (1.0 + t_now[0])
+        for k in range(5):
+            part_row[k, :, :] += closed[:, k * 128 : (k + 1) * 128]
+
+    wide_top = lax.broadcasted_iota(I32, (8, ROWS), 0) < 4
     s_now, t_now = [None], [None]
 
-    @pl.loop(first, 3)
-    def _(s):
+    @pl.loop(0, last)
+    def _(turn):
+        s = (turn + 2) % 3
+
         @pl.when((s < 2) | jnp.logical_not(rhs_is_own))
         def _():
             arrived(s)
@@ -187,43 +208,18 @@
             unpack(s, i, put)
 
         arrived(3 + 2 * s + g)
+
+        @pl.when(turn + 1 < last)
+        def _():
+            pass_on(turn)
+
         s_now[0] = s
-        t_now[0] = jnp.where(s == 0, kinds % 2, jnp.where(s == 1, kinds // 2 % 2, kind))
+        t_now[0] = jnp.where(
+            s == 0, kinds % 2, jnp.where(s == 1, kinds // 2 % 2, kind)
+        ).astype(F32)
         product(0, 3)
 
-        @pl.when(s < 2)
-        def _():
-            pass_on(s + 1)
-
         product(3, 5)
-
-    def fold(i, closed):
-        words = own[pl.ds(pl.multiple_of(i * 8, 8), 8), :]
-        once, twice = closed
-        for q in range(2):
-            part = halves(words[4 * q : 4 * q + 4], wide_top)
-            sums = []
-            for k in range(16):
-                at = pl.ds(pl.multiple_of(i * 256 + q * 128 + k * 8, 8), 8)
-                bit = (part & (1 << k)) != 0
-                a = jnp.where(bit, acc[0, at, :], 0.0)
-                b = jnp.where(bit, acc[1, at, :], 0.0)
-                once, twice = once + a, twice + b
-                a = sum(a[:, k * 128 : (k + 1) * 128] for k in range(5))
-                b = sum(b[:, k * 128 : (k + 1) * 128] for k in range(5))
-                sums.append(2.0 * a + b)
-            across = jnp.concatenate(sums, axis=0).T
-            part_col[2 * i + q, :, :] = jnp.sum(across, axis=0, keepdims=True)
-        return once, twice
-
-    wide_top = lax.broadcasted_iota(I32, (8, ROWS), 0) < 4
-    degree = jnp.sum(lax.population_count(own[...]), axis=0, keepdims=True).astype(F32)
-    zeros = jnp.zeros((8, ROWS), F32)
-    once, twice = lax.fori_loop(0, 5, fold, (zeros, zeros))
-    closed = jnp.sum(once + 2.0 * twice, axis=0, keepdims=True)
-    for k in range(5):
-        part_row[k, :, :] = closed[:, k * 128 : (k + 1) * 128]
-        part_row[5 + k, :, :] = degree[:, k * 128 : (k + 1) * 128]
 
     give_row = [
         copy(part_row, red_row.at[C, h], send.at[7 + k], row_sem.at[C, h], 2 * R + k, R)
@@ -306,9 +302,9 @@
         there, c = offer(i)
         pl.when(there)(c.wait_send)
 
-    @pl.loop(first, 3)
-    def _(s):
-        relay(s).wait_send()
+    @pl.loop(0, last)
+    def _(turn):
+        relay((turn + 2) % 3).wait_send()
 
     @pl.when(off)
     def _():
@@ -353,7 +349,6 @@
             vmem((9, WORDS, ROWS), I32),
             vmem((WIDE, ROWS), F8),
             vmem((WIDE, WIDE), F8),
-            vmem((2, WIDE, ROWS), F32),
             vmem((10, 1, 128), F32),
             vmem((10, 1, 128), F32),
             vmem((8, 2, 10, 1, 128), F32),

time: 37.4 us -> 35.5 us (0.949)
  Pallas kernels: 33.7 us -> 31.8 us
    pallas_call x1, Pallas kernels: 33.7 us -> 31.8 us  [body(): pl.pallas_call(kernel, out_shape=(jax.ShapeDtypeStruct((1, 80), F32), jax...]
where the time goes in v7:
time: 35.5 us; the launch traced here: 35.4 us
  Pallas kernels  31.8 us (90%)
  between operations  2.41 us (7%)
  local copies, waits for them, and re-layouts  1.13 us (3%)
    pallas_call x1, Pallas kernels, body(): pl.pallas_call(kernel, out_shape=(jax.ShapeDtypeStruct((1, 80), F32), jax...  31.8 us
    unnamed x3, local copies, waits for them, and re-layouts  1.13 us

profile of v7, /device:TPU:1, one launch (start us, length us, event | category | flops | bytes accessed | tf_op | source)
XLA Modules:
  0.0 35.4 jit_solution(9570789384632240828)
XLA Ops:
  0.6 31.8 %shard_map.41 = (f32[1,80]{1,0:T(1,128)}, f32[1,1]{1,0:T(1,128)}) custom-call(s32[40,640]{1,0:T(8,128)} %bitcast.4, s32[1,80]{1,0:T(1,128)} %bitcast.5), custom_call_target="tpu_custom_call" | custom-call | tf_op jit(solution)/shard_map/pallas_call | solution.py:341
  32.5 0.0 copy-start
  32.5 0.6 %copy-done = f32[1,80]{1,0:T(1,128)S(1)} copy-done((f32[1,80]{1,0:T(1,128)S(1)}, f32[1,80]{1,0:T(1,128)}, u32[]{:S(2)}) %copy-start) | copy-done | bytes 344
  33.1 0.5 %copy.6 = f32[80]{0:T(128)} copy(f32[80]{0:T(128)S(1)} %bitcast.6) | data formatting | bytes 640
Async XLA Ops:
  32.5 0.6 %copy-start = (f32[1,80]{1,0:T(1,128)S(1)}, f32[1,80]{1,0:T(1,128)}, u32[]{:S(2)}) copy-start(f32[1,80]{1,0:T(1,128)} %get-tuple-element.4) | copy-start | bytes 964

commit v8 on v7

--- a/solution.py
+++ b/solution.py
@@ -368,7 +368,7 @@
             dma((8,)),
         ],
         compiler_params=pltpu.CompilerParams(
-            collective_id=0, has_side_effects=True, vmem_limit_bytes=67043328
+            collective_id=0, has_side_effects=True, vmem_limit_bytes=56551552
         ),
     )(adjacency.T, relabel[None, :])
     return out[0], ratio[0, 0]

time: 35.5 us -> 34.7 us (0.977)
  local copies, waits for them, and re-layouts: 1.13 us -> 0.51 us
    unnamed x3 -> x1, local copies, waits for them, and re-layouts: 1.13 us -> 0.51 us
where the time goes in v8:
time: 34.7 us; the launch traced here: 34.6 us
  Pallas kernels  31.8 us (92%)
  between operations  2.33 us (7%)
  local copies, waits for them, and re-layouts  0.51 us (1%)
    pallas_call x1, Pallas kernels, body(): pl.pallas_call(kernel, out_shape=(jax.ShapeDtypeStruct((1, 80), F32), jax...  31.8 us

profile of v8, /device:TPU:1, one launch (start us, length us, event | category | flops | bytes accessed | tf_op | source)
XLA Modules:
  0.0 34.6 jit_solution(9107131192394720309)
XLA Ops:
  0.6 31.8 %shard_map.41 = (f32[1,80]{1,0:T(1,128)S(1)}, f32[1,1]{1,0:T(1,128)}) custom-call(s32[40,640]{1,0:T(8,128)} %bitcast.5, s32[1,80]{1,0:T(1,128)} %bitcast.6), custom_call_target="tpu_custom_call" | custom-call | tf_op jit(solution)/shard_map/pallas_call | solution.py:341
  32.4 0.5 %copy.6 = f32[80]{0:T(128)} copy(f32[80]{0:T(128)S(1)} %bitcast.4) | data formatting | bytes 640

commit v9 on v8

--- a/solution.py
+++ b/solution.py
@@ -201,18 +201,16 @@
         def _():
             arrived(s)
 
-        @pl.loop(0, 5)
-        def _(i):
+        for i in range(5):
             def put(r, c, piece):
-                w_rhs[pl.ds(pl.multiple_of(i * 256 + r, 32), 32), c : c + 128] = piece
+                w_rhs[i * 256 + r : i * 256 + r + 32, c : c + 128] = piece
             unpack(s, i, put)
-
-        arrived(3 + 2 * s + g)
 
         @pl.when(turn + 1 < last)
         def _():
             pass_on(turn)
 
+        arrived(3 + 2 * s + g)
         s_now[0] = s
         t_now[0] = jnp.where(
             s == 0, kinds % 2, jnp.where(s == 1, kinds // 2 % 2, kind)
@@ -313,6 +311,10 @@
 
     pl.when(diag)(to_other.wait_send)
 
+    @pl.when(diag)
+    def _():
+        for_all(lambda c: c.wait_send())
+
     found = jnp.zeros((11, 128), F32)
     sums = jnp.zeros((1, 128), F32)
     for b in range(8):
@@ -329,10 +331,6 @@
     bottom = jnp.sum(jnp.where(low, 0.0, sums), axis=1, keepdims=True)
     ratio_out[...] = top / bottom
     out[...] = jnp.sum(found, axis=0, keepdims=True)[:, 0:80]
-
-    @pl.when(diag)
-    def _():
-        for_all(lambda c: c.wait_send())
 
 
 def body(adjacency, relabel):

time: 34.7 us -> 34.5 us (level)
  no operation moved by 1% of the time
where the time goes in v9:
time: 34.5 us; the launch traced here: 34.4 us
  Pallas kernels  31.5 us (91%)
  between operations  2.33 us (7%)
  local copies, waits for them, and re-layouts  0.51 us (1%)
    pallas_call x1, Pallas kernels, body(): pl.pallas_call(kernel, out_shape=(jax.ShapeDtypeStruct((1, 80), F32), jax...  31.5 us

profile of v9, /device:TPU:1, one launch (start us, length us, event | category | flops | bytes accessed | tf_op | source)
XLA Modules:
  0.0 34.4 jit_solution(4162941320944905523)
XLA Ops:
  0.6 31.5 %shard_map.41 = (f32[1,80]{1,0:T(1,128)S(1)}, f32[1,1]{1,0:T(1,128)}) custom-call(s32[40,640]{1,0:T(8,128)} %bitcast.5, s32[1,80]{1,0:T(1,128)} %bitcast.6), custom_call_target="tpu_custom_call" | custom-call | tf_op jit(solution)/shard_map/pallas_call | solution.py:339
  32.2 0.5 %copy.6 = f32[80]{0:T(128)} copy(f32[80]{0:T(128)S(1)} %bitcast.4) | data formatting | bytes 640

commit v10 on v8

--- a/solution.py
+++ b/solution.py
@@ -243,7 +243,7 @@
 
     def for_all(act):
         where = [(x, y, z) for x in range(4) for y in range(4) for z in range(4)]
-        where.sort(key=lambda v: sum(min(a, 4 - a) for a in v))
+        where.sort(key=lambda v: min(v[0], 4 - v[0]) + min(v[1], 4 - v[1]) + v[2])
         for x, y, z in where:
             r, c = y * 4 + x % 2 * 2 + h, x // 2 * 4 + z
 
@@ -313,6 +313,10 @@
 
     pl.when(diag)(to_other.wait_send)
 
+    @pl.when(diag)
+    def _():
+        for_all(lambda c: c.wait_send())
+
     found = jnp.zeros((11, 128), F32)
     sums = jnp.zeros((1, 128), F32)
     for b in range(8):
@@ -329,10 +333,6 @@
     bottom = jnp.sum(jnp.where(low, 0.0, sums), axis=1, keepdims=True)
     ratio_out[...] = top / bottom
     out[...] = jnp.sum(found, axis=0, keepdims=True)[:, 0:80]
-
-    @pl.when(diag)
-    def _():
-        for_all(lambda c: c.wait_send())
 
 
 def body(adjacency, relabel):

time: 34.7 us -> 34.6 us (level)
  no operation moved by 1% of the time
where the time goes in v10:
time: 34.6 us; the launch traced here: 34.5 us
  Pallas kernels  31.7 us (92%)
  between operations  2.33 us (7%)
  local copies, waits for them, and re-layouts  0.51 us (1%)
    pallas_call x1, Pallas kernels, body(): pl.pallas_call(kernel, out_shape=(jax.ShapeDtypeStruct((1, 80), F32), jax...  31.7 us

profile of v10, /device:TPU:1, one launch (start us, length us, event | category | flops | bytes accessed | tf_op | source)
XLA Modules:
  0.0 34.5 jit_solution(9168474983033464595)
XLA Ops:
  0.6 31.7 %shard_map.41 = (f32[1,80]{1,0:T(1,128)S(1)}, f32[1,1]{1,0:T(1,128)}) custom-call(s32[40,640]{1,0:T(8,128)} %bitcast.5, s32[1,80]{1,0:T(1,128)} %bitcast.6), custom_call_target="tpu_custom_call" | custom-call | tf_op jit(solution)/shard_map/pallas_call | solution.py:341
  32.3 0.5 %copy.6 = f32[80]{0:T(128)} copy(f32[80]{0:T(128)S(1)} %bitcast.4) | data formatting | bytes 640
